TPU v7x, 32 devices: a whole 2x2x4 slice. The times are simulated.
32 devices in a mesh: gz: 16 (over z, x, core), xy: 2 (over y).
Axes of the slice: x: 2, y: 2, z: 4, core: 2. Of those that a mesh axis runs over, the one named last changes fastest.
Arguments:
- coords: float32 [3, 32, 4, 128], P(None, 'gz', 'xy'), may hold values from 0 to 1
- species: int32 [32, 4, 128], P('gz', 'xy'), may hold values from 0 to 7
- centers: int32 [32, 4, 128], P('gz', 'xy'), may hold values from 0 to 127
- others: int32 [32, 4, 128], P('gz', 'xy'), may hold values from 0 to 1151
- live_count: int32 [32, 4], P('gz', 'xy'), may hold values from 42 to 128
- in_weight: float32 [24, 128], replicated, may hold values from -1.25 to 1.25
- env_weight: float32 [128, 32], replicated, may hold values from -0.5 to 0.5
- up_weight: float32 [160, 128], replicated, may hold values from -0.5 to 0.5
- out_weight: float32 [128], replicated, may hold values from -0.5 to 0.5
Outputs:
- atom_energy: float32 [32, 4, 128], P('gz', 'xy')
- forces: float32 [3, 32, 4, 128], P(None, 'gz', 'xy')
Inputs may be any that keep to these rules, and one draw needn't show every extreme that they name: Edge slots at or after live_count of a bin are padding; at most 128 are live.
All inputs are finite; a program needn't handle non-finite values.
Results may differ from a plain program's by a relative error of at most 0.0018.
Values may be sent and summed in bfloat16 or wider, within the bound.
A program may use at most 64 MiB of HBM per device.

v0:
```python
import functools
import math

import jax
import jax.numpy as jnp
from jax import lax
from jax.experimental import pallas as pl
from jax.experimental.pallas import tpu as pltpu
from jax.sharding import PartitionSpec as P

SOFTEN = 0.01
CUTOFF = 3.5
F32 = jnp.float32
BF16 = jnp.bfloat16
MESH = pl.DeviceIdType.MESH


def rounded(x):
    return x.astype(BF16).astype(F32)


def split(x):
    high = x.astype(BF16)
    return high, (x - high.astype(F32)).astype(BF16)


def dot(a, b):
    return jnp.dot(a, b, preferred_element_type=F32)


def dot_t(a, b):
    return lax.dot_general(a, b, (((1,), (1,)), ((), ())), preferred_element_type=F32)


def join(parts, axis):
    return parts[0] if len(parts) == 1 else jnp.concatenate(parts, axis=axis)


def neighbours(nz, nx):
    slots = {(0, 0): 0}
    for dz in (-1, 0, 1):
        for dx in (-1, 0, 1):
            slots.setdefault((dz % nz, dx % nx), len(slots))
    return slots


def kernel(
    nz, nx, bz, bx, nb, spec, ch, lat,
    coords_hbm, species_hbm, centers_hbm, others_hbm, live_hbm, in_hbm, env_hbm, up_hbm, out_hbm,
    result_ref,
    coords_ref, species_ref, centers_ref, others_ref, live_ref, in_ref, env_ref, up_ref, out_ref,
    own, halo, tab, ct, ot, rows_live, rows_p, geo, xs, sins, coss, rad, harm,
    l2, dsilu, wts, feat, dfeat, dlat_own, env_grad, dharm, drad, gr, grad, back,
    send1, recv1, send2, recv2, load_sem,
):
    n = coords_ref.shape[-1]
    slots = neighbours(nz, nx)
    me_z, me_x = lax.axis_index("gz"), lax.axis_index("xy")
    others_list = [(key, s) for key, s in slots.items() if s > 0]

    def device(key):
        return (lax.rem(me_z + key[0], nz), lax.rem(me_x + key[1], nx))

    def mirror(key):
        return slots[((-key[0]) % nz, (-key[1]) % nx)]

    barrier = pltpu.get_barrier_semaphore()
    for key, _ in others_list:
        pl.semaphore_signal(barrier, inc=1, device_id=device(key), device_id_type=MESH)

    loads = [
        pltpu.make_async_copy(source, target, load_sem.at[k])
        for k, (source, target) in enumerate([
            (coords_hbm, coords_ref), (species_hbm, species_ref), (centers_hbm, centers_ref),
            (others_hbm, others_ref), (live_hbm, live_ref), (in_hbm, in_ref), (env_hbm, env_ref),
            (up_hbm, up_ref), (out_hbm, out_ref)])
    ]
    for load in loads:
        load.start()
    for load in loads[:5]:
        load.wait()
    lane = lax.broadcasted_iota(jnp.int32, (1, n), 1)
    for a in range(bz):
        for b in range(bx):
            alive = (lane < live_ref[a : a + 1, b : b + 1]).astype(F32)
            own[a, b] = jnp.concatenate(
                [
                    coords_ref[:, a, b, :],
                    species_ref[a, b : b + 1, :].astype(F32),
                    centers_ref[a, b : b + 1, :].astype(F32),
                    others_ref[a, b : b + 1, :].astype(F32),
                    alive,
                    jnp.zeros((1, n), F32),
                ],
                axis=0,
            )
    pl.semaphore_wait(barrier, len(others_list))
    first = []
    for key, s in others_list:
        t = mirror(key)
        copy = pltpu.make_async_remote_copy(
            src_ref=own, dst_ref=halo.at[t - 1], send_sem=send1.at[s - 1],
            recv_sem=recv1.at[t - 1], device_id=device(key), device_id_type=MESH,
        )
        copy.start()
        first.append(copy)

    for load in loads[5:]:
        load.wait()
    w_in = in_ref[...]
    w_hi = rounded(w_in)
    w_lo = w_in - w_hi
    w_rows = jnp.concatenate(
        [w_hi[:nb], w_lo[:nb], w_hi[:nb], w_hi[nb:], w_lo[nb:],
         jnp.zeros((lat - 3 * nb - 4 * spec, lat), F32)], axis=0)
    kin = (3 * nb + 4 * spec + 15) // 16 * 16
    in_t = w_rows.T.astype(BF16)[:, :kin]
    pad8 = jnp.zeros((nb, lat), F32)
    wr_hi = jnp.concatenate([w_hi[:nb], pad8], axis=0).astype(BF16)
    wr_lo = jnp.concatenate([w_lo[:nb], pad8], axis=0).astype(BF16)
    wr3 = jnp.concatenate([wr_hi, wr_hi, wr_lo], axis=1)
    env_t = env_ref[...]
    et_hi = rounded(env_t)
    et_lo = env_t - et_hi
    env_t3 = jnp.concatenate([et_hi, et_hi, et_lo], axis=1).astype(BF16)
    kpad = -(3 * ch) % lat
    env3 = jnp.concatenate(
        [et_hi, et_hi, et_lo] + ([jnp.zeros((kpad, lat), F32)] if kpad else []), axis=0
    ).T.astype(BF16)
    up = up_ref[...]
    up_hi = rounded(up)
    up_lo = up - up_hi
    up3 = jnp.concatenate([up_hi, up_hi, up_lo], axis=1).astype(BF16)
    up_t = jnp.concatenate(
        [x.T.astype(BF16) for x in (up_hi[:lat], up_hi[:lat], up_lo[:lat])]
        + [jnp.concatenate(
            [up_hi[lat:], up_hi[lat:], up_lo[lat:]]
            + ([jnp.zeros((kpad, lat), F32)] if kpad else []), axis=0).T.astype(BF16)],
        axis=1)
    out_col = jnp.broadcast_to(out_ref[...], (n, lat)).T

    cells = [(a, b) for a in range(bz - 1, 2 * bz + 1) for b in range(bx - 1, 2 * bx + 1)]
    row_n = lax.broadcasted_iota(jnp.int32, (n, n), 0)

    def hots_of(i, part):
        o = part[5:6].astype(jnp.int32)
        ct[i] = (row_n == part[4:5].astype(jnp.int32)).astype(F32).astype(BF16)
        ot[i] = (row_n == (o & 127)).astype(F32).astype(BF16)

    mine = [i for i, (a, b) in enumerate(cells) if bz <= a < 2 * bz and bx <= b < 2 * bx]
    for i in mine:
        hots_of(i, own[cells[i][0] - bz, cells[i][1] - bx])
    for copy in first:
        copy.wait()

    def place(a, b):
        return slots[((a // bz - 1) % nz, (b // bx - 1) % nx)], a % bz, b % bx

    def block(a, b):
        s, i, j = place(a, b)
        return own[i, j] if s == 0 else halo[s - 1, i, j]

    window_z = range(bz - 2, 2 * bz + 2)
    window_x = range(bx - 2, 2 * bx + 2)
    for a in window_z:
        for b in window_x:
            part = block(a, b)
            hi = rounded(part)
            tab[a, b] = jnp.concatenate([hi, part - hi], axis=0).astype(BF16)

    cx = bx + 2
    total = len(cells)
    row_s = lax.broadcasted_iota(jnp.int32, (spec, n), 0).astype(F32)
    for i, (a, b) in enumerate(cells):
        part = block(a, b)
        o = part[5:6].astype(jnp.int32)
        p = o >> 7
        if i not in mine:
            hots_of(i, part)
        hot_c, hot_o = ct[i], ot[i]
        at_c = dot(tab[a, b], hot_c)
        at_c = at_c[:8] + at_c[8:]
        around = jnp.concatenate(
            [tab[a + dz, b + dx] for dz in (-1, 0, 1) for dx in (-1, 0, 1)], axis=0)
        got = dot(around, hot_o)
        at_o = jnp.zeros((8, n), F32)
        for off in range(9):
            at_o = jnp.where(p == off, got[16 * off : 16 * off + 8] + got[16 * off + 8 : 16 * off + 16], at_o)
        diff = at_o - at_c
        up3_ = (p >= 3).astype(jnp.int32) + (p >= 6).astype(jnp.int32)
        geo[0, i : i + 1] = diff[0:1] + (up3_ - 1).astype(F32)
        geo[1, i : i + 1] = diff[1:2] + (p - 3 * up3_ - 1).astype(F32)
        geo[2, i : i + 1] = diff[2:3]
        xs[:spec, i * n : (i + 1) * n] = (row_s == at_c[3:4]).astype(F32)
        xs[spec:, i * n : (i + 1) * n] = (row_s == at_o[3:4]).astype(F32)
        rows_live[i : i + 1] = part[6:7]
        rows_p[i : i + 1] = p

    r = [geo[m] for m in range(3)]
    dist = jnp.sqrt(r[0] * r[0] + r[1] * r[1] + r[2] * r[2] + SOFTEN)
    inv = 1.0 / dist
    q = dist / CUTOFF
    rest = 1.0 - q * q
    envelope = rest * rest
    scale = inv * envelope
    s1 = jnp.sin(math.pi * q)
    c1 = jnp.cos(math.pi * q)
    s0, c0, sk, ck = jnp.zeros_like(s1), jnp.ones_like(c1), s1, c1
    for k in range(nb):
        sins[k] = sk
        coss[k] = ck
        rad[k] = sk * scale
        s0, sk = sk, 2.0 * c1 * sk - s0
        c0, ck = ck, 2.0 * c1 * ck - c0
    for m in range(3):
        harm[m] = r[m] * inv
    env_grad[...] = jnp.zeros_like(env_grad)
    geo[3] = envelope

    interior = {}
    for i, (a, b) in enumerate(cells):
        if bz <= a < 2 * bz and bx <= b < 2 * bx:
            interior[i] = (a - bz) * bx + (b - bx)

    group = 4 if total % 4 == 0 else 1
    for g in range(0, total, group):
        ids = list(range(g, g + group))
        span = slice(g * n, (g + group) * n)
        radial = join([rad[:, i, :] for i in ids], 1)
        rh = rounded(radial)
        x_s = xs[:, span]
        parts = [rh, rh, radial - rh, x_s, x_s]
        fill = kin - 3 * nb - 4 * spec
        if fill:
            parts.append(jnp.zeros((fill, group * n), F32))
        pre = dot(in_t, jnp.concatenate(parts, axis=0).astype(BF16))
        sig = 1.0 / (1.0 + jnp.exp(-pre))
        latent = pre * sig
        dsilu[:, span] = sig + latent * (1.0 - sig)
        lh, ll = split(latent)
        for t, i in enumerate(ids):
            if i in interior:
                l2[interior[i], 0] = lh[:, t * n : (t + 1) * n]
                l2[interior[i], 1] = ll[:, t * n : (t + 1) * n]
        alive = join([rows_live[i : i + 1] for i in ids], 1)
        w = dot(env_t3, jnp.concatenate([lh, ll, lh], axis=0)) * alive
        wts[:, span] = w
        msgs = jnp.concatenate(
            [w] + [w * join([harm[m, i : i + 1] for i in ids], 1) for m in range(3)], axis=0)
        mh, ml = split(msgs)
        for t, i in enumerate(ids):
            cut = slice(t * n, (t + 1) * n)
            hot_c = ct[i]
            feat[:, i * n : (i + 1) * n] = dot_t(
                jnp.concatenate([mh[:, cut], ml[:, cut]], axis=1),
                jnp.concatenate([hot_c, hot_c], axis=1)).astype(BF16)

    dfeat[...] = jnp.zeros_like(dfeat)
    row_8 = lax.broadcasted_iota(jnp.int32, (16, n), 0)
    for i, k in interior.items():
        hot_c, hot_o = ct[i], ot[i]
        p = rows_p[i : i + 1]
        env_row = geo[3, i : i + 1]
        alive = rows_live[i : i + 1]
        f_c = dot(feat[:, i * n : (i + 1) * n], hot_c)
        f_o = None
        hots = []
        for dz in range(3):
            start = i + (dz - 1) * cx - 1
            hot3 = jnp.concatenate(
                [hot_o * (p == 3 * dz + dx).astype(F32).astype(BF16) for dx in range(3)], axis=0)
            hots.append((start, hot3))
            term = dot(feat[:, start * n : (start + 3) * n], hot3)
            f_o = term if f_o is None else f_o + term
        prod4 = f_c * f_o
        prod = prod4[:ch] + prod4[ch : 2 * ch] + prod4[2 * ch : 3 * ch] + prod4[3 * ch :]
        ph, pl_ = split(prod)
        parts = [l2[k, 0], l2[k, 1], l2[k, 0], ph, pl_, ph]
        if kpad:
            parts.append(jnp.zeros((kpad, n), BF16))
        u = dot(up_t, jnp.concatenate(parts, axis=0))
        sig = 1.0 / (1.0 + jnp.exp(-u))
        hid = u * sig
        raw = jnp.sum(out_col * hid, axis=0, keepdims=True) * alive
        env_grad[i : i + 1] = raw
        e_row = raw * env_row
        e_hi = rounded(e_row)
        e_rows = jnp.where(row_8 == 0, e_hi, jnp.where(row_8 == 1, e_row - e_hi, 0.0)).astype(BF16)
        e_atom = dot_t(e_rows, hot_c)
        result_ref[3, k // bx, k % bx : k % bx + 1, :] = e_atom[0:1] + e_atom[1:2]
        d_u = out_col * (alive * env_row) * (sig + hid * (1.0 - sig))
        dh, dl = split(d_u)
        d_join = dot(up3, jnp.concatenate([dh, dl, dh], axis=0))
        dlat_own[k] = d_join[:lat]
        d_prod = jnp.concatenate([d_join[lat:]] * 4, axis=0)
        dch, dcl = split(d_prod * f_o)
        doh, dol = split(d_prod * f_c)
        dfeat[:, i * n : (i + 1) * n] += dot_t(
            jnp.concatenate([dch, dcl], axis=1), jnp.concatenate([hot_c, hot_c], axis=1))
        d_o = jnp.concatenate([doh, dol], axis=1)
        for start, hot3 in hots:
            dfeat[:, start * n : (start + 3) * n] += dot_t(
                d_o, jnp.concatenate([hot3, hot3], axis=1))

    for g in range(0, total, group):
        ids = list(range(g, g + group))
        span = slice(g * n, (g + group) * n)
        dm = []
        for i in ids:
            hot_c = ct[i]
            fh, fl = split(dfeat[:, i * n : (i + 1) * n])
            dm.append(dot(jnp.concatenate([fh, fl], axis=1), jnp.concatenate([hot_c, hot_c], axis=0)))
        dm = join(dm, 1)
        w = wts[:, span]
        dw = dm[:ch]
        for m in range(3):
            piece = dm[(m + 1) * ch : (m + 2) * ch]
            dw = dw + piece * join([harm[m, i : i + 1] for i in ids], 1)
            d_h = jnp.sum(piece * w, axis=0, keepdims=True)
            for t, i in enumerate(ids):
                dharm[m, i : i + 1] = d_h[:, t * n : (t + 1) * n]
        dw = dw * join([rows_live[i : i + 1] for i in ids], 1)
        wh, wl = split(dw)
        parts = [wh, wl, wh]
        if kpad:
            parts.append(jnp.zeros((kpad, group * n), BF16))
        d_lat = dot(env3, jnp.concatenate(parts, axis=0))
        if any(i in interior for i in ids):
            d_lat = d_lat + join(
                [dlat_own[interior[i]] if i in interior else jnp.zeros((lat, n), F32) for i in ids], 1)
        dh, dl = split(d_lat * dsilu[:, span])
        d_r = dot(wr3, jnp.concatenate([dh, dl, dh], axis=0))
        for t, i in enumerate(ids):
            drad[:, i, :] = d_r[:nb, t * n : (t + 1) * n]

    sum_s = drad[0] * sins[0]
    sum_c = drad[0] * coss[0]
    for k in range(1, nb):
        sum_s = sum_s + drad[k] * sins[k]
        sum_c = sum_c + (k + 1.0) * (drad[k] * coss[k])
    env_slope = (-4.0 / CUTOFF) * q * rest
    d_dist = (
        (math.pi / CUTOFF) * sum_c * scale
        - sum_s * scale * inv
        + (sum_s * inv + env_grad[...]) * env_slope
    )
    for m in range(3):
        d_dist = d_dist - dharm[m] * r[m] * (inv * inv)
    gr[...] = jnp.zeros_like(gr)
    for m in range(3):
        d_m = d_dist * harm[m] + dharm[m] * inv
        hi = rounded(d_m)
        gr[:, m, :] = hi
        gr[:, m + 4, :] = d_m - hi

    grad[...] = jnp.zeros_like(grad)
    second = {}

    def give(ready):
        for key, s in others_list:
            if s in second or not ready(s):
                continue
            t = mirror(key)
            second[s] = pltpu.make_async_remote_copy(
                src_ref=grad.at[s], dst_ref=back.at[t - 1], send_sem=send2.at[s - 1],
                recv_sem=recv2.at[t - 1], device_id=device(key), device_id_type=MESH,
            )
            second[s].start()

    order = sorted(range(total), key=lambda i: (-cells[i][0], cells[i][1]))
    targets = [
        {place(cells[i][0] + dz, cells[i][1] + dx)[0] for dz in (-1, 0, 1) for dx in (-1, 0, 1)}
        for i in order]
    for turn, i in enumerate(order):
        a, b = cells[i]
        g8 = gr[i]
        p = rows_p[i : i + 1]
        at_c = dot_t(jnp.concatenate([g8, jnp.zeros_like(g8)], axis=0).astype(BF16), ct[i])
        stack = [jnp.where(p == off, g8, 0.0) for off in range(9)] + [jnp.zeros_like(g8)]
        at_o = dot_t(jnp.concatenate(stack, axis=0).astype(BF16), ot[i])
        s, y, x = place(a, b)
        grad[s, y, x] -= at_c[:8]
        for off in range(9):
            s, y, x = place(a + off // 3 - 1, b + off % 3 - 1)
            grad[s, y, x] += at_o[8 * off : 8 * off + 8]
        if turn + 1 < total and b == cells[-1][1]:
            later = set().union(*targets[turn + 1 :])
            give(lambda s: s not in later)
    give(lambda s: True)
    for copy in second.values():
        copy.wait()
    for a in range(bz):
        for b in range(bx):
            acc = grad[0, a, b]
            for s in range(len(others_list)):
                acc = acc + back[s, a, b]
            acc = -(acc[:4] + acc[4:])
            result_ref[:3, a, b, :] = acc[:3]


def solution(mesh):
    nz, nx = mesh.shape["gz"], mesh.shape["xy"]

    def body(coords, species, centers, others, live_count, in_weight, env_weight, up_weight, out_weight):
        _, bz, bx, n = coords.shape
        lat, ch = env_weight.shape
        nb = 8
        spec = (in_weight.shape[0] - nb) // 2
        cells = (bz + 2) * (bx + 2)
        ns = len(neighbours(nz, nx)) - 1
        vmem = lambda shape, dtype=F32: pltpu.VMEM(shape, dtype)
        args = (coords, species, centers, others, live_count, in_weight, env_weight.T, up_weight,
                out_weight[None])
        scratch = [vmem(x.shape, x.dtype) for x in args] + [
            vmem((bz, bx, 8, n)),
            vmem((ns, bz, bx, 8, n)),
            vmem((3 * bz, 3 * bx, 16, n), BF16),
            vmem((cells, n, n), BF16),
            vmem((cells, n, n), BF16),
            vmem((cells, n)),
            vmem((cells, n), jnp.int32),
            vmem((4, cells, n)),
            vmem((2 * spec, cells * n)),
            vmem((nb, cells, n)),
            vmem((nb, cells, n)),
            vmem((nb, cells, n)),
            vmem((3, cells, n)),
            vmem((bz * bx, 2, lat, n), BF16),
            vmem((lat, cells * n)),
            vmem((ch, cells * n)),
            vmem((4 * ch, cells * n), BF16),
            vmem((4 * ch, cells * n)),
            vmem((bz * bx, lat, n)),
            vmem((cells, n)),
            vmem((3, cells, n)),
            vmem((nb, cells, n)),
            vmem((cells, 8, n)),
            vmem((ns + 1, bz, bx, 8, n)),
            vmem((ns, bz, bx, 8, n)),
        ] + [pltpu.SemaphoreType.DMA((ns,)) for _ in range(4)]
        scratch.append(pltpu.SemaphoreType.DMA((len(args),)))
        specs = [pl.BlockSpec(memory_space=pl.ANY) for _ in args]
        result = pl.pallas_call(
            functools.partial(kernel, nz, nx, bz, bx, nb, spec, ch, lat),
            out_shape=pltpu.VMEM((4, bz, bx, n), F32),
            in_specs=specs,
            out_specs=pl.BlockSpec(memory_space=pltpu.VMEM),
            scratch_shapes=scratch,
            compiler_params=pltpu.CompilerParams(collective_id=0, has_side_effects=True),
        )(*args)
        return result[3], result[:3]

    in_specs = (
        P(None, "gz", "xy", None), P("gz", "xy", None), P("gz", "xy", None), P("gz", "xy", None),
        P("gz", "xy"), P(), P(), P(), P(),
    )
    out_specs = (P("gz", "xy", None), P(None, "gz", "xy", None))
    return jax.shard_map(body, mesh=mesh, in_specs=in_specs, out_specs=out_specs, check_vma=False)
```

profile of v0, /device:TPU:0, one launch (start us, length us, event | category | flops | bytes accessed | tf_op | source)
XLA Modules:
  0.0 24.3 jit_solution(13469473088916171576)
XLA Ops:
  0.6 22.4 %shard_map.104 = f32[4,2,2,128]{3,2,1,0:T(2,128)S(1)} custom-call(f32[3,2,2,128]{3,2,1,0:T(2,128)} %coords_hbm.1, s32[2,2,128]{2,1,0:T(2,128)} %species_hbm.1, s32[2,2,128]{2,1,0:T(2,128)} %centers_hbm.1, s32[2,2,128]{2,1,0:T(2,128)} %others_hbm.1, s32[2,2]{1,0:T(2,128)} %live_hbm.1, f32[24,128]{1,0:T(8,128)} %in_hbm.1, f32[32,128]{1,0:T(8,128)} %bitcast.4, ...), custom_call_target="tpu_custom_call" | custom-call | tf_op jit(solution)/shard_map/pallas_call | solution.py:443
  23.1 0.6 %slice_bitcast_fusion = f32[2,2,128]{2,1,0:T(2,128)} fusion(f32[4,2,2,128]{3,2,1,0:T(2,128)S(1)} %shard_map.104), kind=kLoop, calls=%fused_computation | loop fusion | bytes 4096 | tf_op jit(solution)/shard_map/squeeze | solution.py:451
  23.7 0.6 %slice.7 = f32[3,2,2,128]{3,2,1,0:T(2,128)} slice(f32[4,2,2,128]{3,2,1,0:T(2,128)S(1)} %shard_map.104), slice={[0:3], [0:2], [0:2], [0:128]} | slice | bytes 12288 | tf_op jit(solution)/shard_map/slice | solution.py:451
where the time goes:
time: 24.5 us; the launch traced here: 24.3 us
  Pallas kernels  22.4 us (91%)
  local copies, waits for them, and re-layouts  1.17 us (5%)
  between operations  0.64 us (3%)
    pallas_call x1, Pallas kernels, body(): pl.pallas_call(functools.partial(kernel, nz, nx, bz, bx, nb, spec, ch, la...  22.4 us
    slice x1, local copies, waits for them, and re-layouts, body(): return (result[3], result[:3])  0.59 us
    squeeze x1, local copies, waits for them, and re-layouts, body(): return (result[3], result[:3])  0.58 us

commit v1 on v0

--- a/solution.py
+++ b/solution.py
@@ -49,24 +49,26 @@
     coords_hbm, species_hbm, centers_hbm, others_hbm, live_hbm, in_hbm, env_hbm, up_hbm, out_hbm,
     result_ref,
     coords_ref, species_ref, centers_ref, others_ref, live_ref, in_ref, env_ref, up_ref, out_ref,
-    own, halo, tab, ct, ot, rows_live, rows_p, geo, xs, sins, coss, rad, harm,
+    halo, tab, ct, ot, rows_live, rows_p, geo, xs, sins, coss, rad, harm,
     l2, dsilu, wts, feat, dfeat, dlat_own, env_grad, dharm, drad, gr, grad, back,
     send1, recv1, send2, recv2, load_sem,
 ):
     n = coords_ref.shape[-1]
     slots = neighbours(nz, nx)
     me_z, me_x = lax.axis_index("gz"), lax.axis_index("xy")
-    others_list = [(key, s) for key, s in slots.items() if s > 0]
-
-    def device(key):
-        return (lax.rem(me_z + key[0], nz), lax.rem(me_x + key[1], nx))
-
-    def mirror(key):
-        return slots[((-key[0]) % nz, (-key[1]) % nx)]
+    mine = slots[(1 % nz, 0)]
+    others_list = [(key, s) for key, s in slots.items() if s != mine]
+    index = {s: i for i, (_, s) in enumerate(others_list)}
+
+    def owner(key):
+        return (lax.rem(me_z + (key[0] - 1) % nz, nz), lax.rem(me_x + key[1], nx))
+
+    def user(key):
+        return (lax.rem(me_z + (1 - key[0]) % nz, nz), lax.rem(me_x + (-key[1]) % nx, nx))
 
     barrier = pltpu.get_barrier_semaphore()
     for key, _ in others_list:
-        pl.semaphore_signal(barrier, inc=1, device_id=device(key), device_id_type=MESH)
+        pl.semaphore_signal(barrier, inc=1, device_id=owner(key), device_id_type=MESH)
 
     loads = [
         pltpu.make_async_copy(source, target, load_sem.at[k])
@@ -83,7 +85,7 @@
     for a in range(bz):
         for b in range(bx):
             alive = (lane < live_ref[a : a + 1, b : b + 1]).astype(F32)
-            own[a, b] = jnp.concatenate(
+            halo[mine, a, b] = jnp.concatenate(
                 [
                     coords_ref[:, a, b, :],
                     species_ref[a, b : b + 1, :].astype(F32),
@@ -97,10 +99,10 @@
     pl.semaphore_wait(barrier, len(others_list))
     first = []
     for key, s in others_list:
-        t = mirror(key)
+        i = index[s]
         copy = pltpu.make_async_remote_copy(
-            src_ref=own, dst_ref=halo.at[t - 1], send_sem=send1.at[s - 1],
-            recv_sem=recv1.at[t - 1], device_id=device(key), device_id_type=MESH,
+            src_ref=halo.at[mine], dst_ref=halo.at[s], send_sem=send1.at[i],
+            recv_sem=recv1.at[i], device_id=user(key), device_id_type=MESH,
         )
         copy.start()
         first.append(copy)
@@ -147,9 +149,6 @@
         ct[i] = (row_n == part[4:5].astype(jnp.int32)).astype(F32).astype(BF16)
         ot[i] = (row_n == (o & 127)).astype(F32).astype(BF16)
 
-    mine = [i for i, (a, b) in enumerate(cells) if bz <= a < 2 * bz and bx <= b < 2 * bx]
-    for i in mine:
-        hots_of(i, own[cells[i][0] - bz, cells[i][1] - bx])
     for copy in first:
         copy.wait()
 
@@ -158,7 +157,7 @@
 
     def block(a, b):
         s, i, j = place(a, b)
-        return own[i, j] if s == 0 else halo[s - 1, i, j]
+        return halo[s, i, j]
 
     window_z = range(bz - 2, 2 * bz + 2)
     window_x = range(bx - 2, 2 * bx + 2)
@@ -175,8 +174,7 @@
         part = block(a, b)
         o = part[5:6].astype(jnp.int32)
         p = o >> 7
-        if i not in mine:
-            hots_of(i, part)
+        hots_of(i, part)
         hot_c, hot_o = ct[i], ot[i]
         at_c = dot(tab[a, b], hot_c)
         at_c = at_c[:8] + at_c[8:]
@@ -256,6 +254,7 @@
                 jnp.concatenate([hot_c, hot_c], axis=1)).astype(BF16)
 
     dfeat[...] = jnp.zeros_like(dfeat)
+    grad[...] = jnp.zeros_like(grad)
     row_8 = lax.broadcasted_iota(jnp.int32, (16, n), 0)
     for i, k in interior.items():
         hot_c, hot_o = ct[i], ot[i]
@@ -287,7 +286,7 @@
         e_hi = rounded(e_row)
         e_rows = jnp.where(row_8 == 0, e_hi, jnp.where(row_8 == 1, e_row - e_hi, 0.0)).astype(BF16)
         e_atom = dot_t(e_rows, hot_c)
-        result_ref[3, k // bx, k % bx : k % bx + 1, :] = e_atom[0:1] + e_atom[1:2]
+        grad[0, k // bx, k % bx, 3:4] = -(e_atom[0:1] + e_atom[1:2])
         d_u = out_col * (alive * env_row) * (sig + hid * (1.0 - sig))
         dh, dl = split(d_u)
         d_join = dot(up3, jnp.concatenate([dh, dl, dh], axis=0))
@@ -353,17 +352,16 @@
         gr[:, m, :] = hi
         gr[:, m + 4, :] = d_m - hi
 
-    grad[...] = jnp.zeros_like(grad)
     second = {}
 
     def give(ready):
         for key, s in others_list:
             if s in second or not ready(s):
                 continue
-            t = mirror(key)
+            i = index[s]
             second[s] = pltpu.make_async_remote_copy(
-                src_ref=grad.at[s], dst_ref=back.at[t - 1], send_sem=send2.at[s - 1],
-                recv_sem=recv2.at[t - 1], device_id=device(key), device_id_type=MESH,
+                src_ref=grad.at[s], dst_ref=back.at[i], send_sem=send2.at[i],
+                recv_sem=recv2.at[i], device_id=owner(key), device_id_type=MESH,
             )
             second[s].start()
 
@@ -391,11 +389,10 @@
         copy.wait()
     for a in range(bz):
         for b in range(bx):
-            acc = grad[0, a, b]
+            acc = grad[mine, a, b]
             for s in range(len(others_list)):
                 acc = acc + back[s, a, b]
-            acc = -(acc[:4] + acc[4:])
-            result_ref[:3, a, b, :] = acc[:3]
+            result_ref[:, a, b, :] = -(acc[:4] + acc[4:])
 
 
 def solution(mesh):
@@ -412,8 +409,7 @@
         args = (coords, species, centers, others, live_count, in_weight, env_weight.T, up_weight,
                 out_weight[None])
         scratch = [vmem(x.shape, x.dtype) for x in args] + [
-            vmem((bz, bx, 8, n)),
-            vmem((ns, bz, bx, 8, n)),
+            vmem((ns + 1, bz, bx, 8, n)),
             vmem((3 * bz, 3 * bx, 16, n), BF16),
             vmem((cells, n, n), BF16),
             vmem((cells, n, n), BF16),

time: 24.5 us -> 22.3 us (0.910)
  Pallas kernels: 22.4 us -> 20.3 us
    pallas_call x1, Pallas kernels: 22.4 us -> 20.3 us  [body(): pl.pallas_call(functools.partial(kernel, nz, nx, bz, bx, nb, spec, ch, la...]
where the time goes in v1:
time: 22.3 us; the launch traced here: 22.1 us
  Pallas kernels  20.3 us (91%)
  local copies, waits for them, and re-layouts  1.17 us (5%)
  between operations  0.64 us (3%)
    pallas_call x1, Pallas kernels, body(): pl.pallas_call(functools.partial(kernel, nz, nx, bz, bx, nb, spec, ch, la...  20.3 us
    slice x1, local copies, waits for them, and re-layouts, body(): return (result[3], result[:3])  0.59 us
    squeeze x1, local copies, waits for them, and re-layouts, body(): return (result[3], result[:3])  0.58 us

profile of v1, /device:TPU:0, one launch (start us, length us, event | category | flops | bytes accessed | tf_op | source)
XLA Modules:
  0.0 22.1 jit_solution(14820380279269340178)
XLA Ops:
  0.6 20.3 %shard_map.104 = f32[4,2,2,128]{3,2,1,0:T(2,128)S(1)} custom-call(f32[3,2,2,128]{3,2,1,0:T(2,128)} %coords_hbm.1, s32[2,2,128]{2,1,0:T(2,128)} %species_hbm.1, s32[2,2,128]{2,1,0:T(2,128)} %centers_hbm.1, s32[2,2,128]{2,1,0:T(2,128)} %others_hbm.1, s32[2,2]{1,0:T(2,128)} %live_hbm.1, f32[24,128]{1,0:T(8,128)} %in_hbm.1, f32[32,128]{1,0:T(8,128)} %bitcast.4, ...), custom_call_target="tpu_custom_call" | custom-call | tf_op jit(solution)/shard_map/pallas_call | solution.py:439
  21.0 0.6 %slice_bitcast_fusion = f32[2,2,128]{2,1,0:T(2,128)} fusion(f32[4,2,2,128]{3,2,1,0:T(2,128)S(1)} %shard_map.104), kind=kLoop, calls=%fused_computation | loop fusion | bytes 4096 | tf_op jit(solution)/shard_map/squeeze | solution.py:447
  21.6 0.6 %slice.7 = f32[3,2,2,128]{3,2,1,0:T(2,128)} slice(f32[4,2,2,128]{3,2,1,0:T(2,128)S(1)} %shard_map.104), slice={[0:3], [0:2], [0:2], [0:128]} | slice | bytes 12288 | tf_op jit(solution)/shard_map/slice | solution.py:447

commit v2 on v1

--- a/solution.py
+++ b/solution.py
@@ -49,7 +49,7 @@
     coords_hbm, species_hbm, centers_hbm, others_hbm, live_hbm, in_hbm, env_hbm, up_hbm, out_hbm,
     result_ref,
     coords_ref, species_ref, centers_ref, others_ref, live_ref, in_ref, env_ref, up_ref, out_ref,
-    halo, tab, ct, ot, rows_live, rows_p, geo, xs, sins, coss, rad, harm,
+    halo, tab, ct, ot, hot_rows, rows_live, rows_p, geo, xs, sins, coss, rad, harm,
     l2, dsilu, wts, feat, dfeat, dlat_own, env_grad, dharm, drad, gr, grad, back,
     send1, recv1, send2, recv2, load_sem,
 ):
@@ -141,16 +141,16 @@
         axis=1)
     out_col = jnp.broadcast_to(out_ref[...], (n, lat)).T
 
+    hot_rows[...] = jnp.zeros_like(hot_rows)
+    grad[...] = jnp.zeros_like(grad)
+    cz, cx = bz + 2, bx + 2
+    total = cz * cx
+    wide = cx * n
+    inner = bx * n
     cells = [(a, b) for a in range(bz - 1, 2 * bz + 1) for b in range(bx - 1, 2 * bx + 1)]
-    row_n = lax.broadcasted_iota(jnp.int32, (n, n), 0)
-
-    def hots_of(i, part):
-        o = part[5:6].astype(jnp.int32)
-        ct[i] = (row_n == part[4:5].astype(jnp.int32)).astype(F32).astype(BF16)
-        ot[i] = (row_n == (o & 127)).astype(F32).astype(BF16)
-
-    for copy in first:
-        copy.wait()
+    row_n = lax.broadcasted_iota(jnp.int32, (n, n), 0).astype(F32).astype(BF16)
+    row_s = lax.broadcasted_iota(jnp.int32, (spec, n), 0).astype(F32)
+    one, zero = jnp.ones((n, n), BF16), jnp.zeros((n, n), BF16)
 
     def place(a, b):
         return slots[((a // bz - 1) % nz, (b // bx - 1) % nx)], a % bz, b % bx
@@ -159,23 +159,29 @@
         s, i, j = place(a, b)
         return halo[s, i, j]
 
-    window_z = range(bz - 2, 2 * bz + 2)
-    window_x = range(bx - 2, 2 * bx + 2)
-    for a in window_z:
-        for b in window_x:
-            part = block(a, b)
-            hi = rounded(part)
-            tab[a, b] = jnp.concatenate([hi, part - hi], axis=0).astype(BF16)
-
-    cx = bx + 2
-    total = len(cells)
-    row_s = lax.broadcasted_iota(jnp.int32, (spec, n), 0).astype(F32)
-    for i, (a, b) in enumerate(cells):
+    def tables(rows):
+        for a in rows:
+            for b in range(bx - 2, 2 * bx + 2):
+                part = block(a, b)
+                hi = rounded(part)
+                tab[a, b] = jnp.concatenate([hi, part - hi], axis=0).astype(BF16)
+
+    def gather(i):
+        a, b = cells[i]
         part = block(a, b)
         o = part[5:6].astype(jnp.int32)
         p = o >> 7
-        hots_of(i, part)
-        hot_c, hot_o = ct[i], ot[i]
+        hot_c = jnp.where(row_n == part[4:5].astype(BF16), one, zero)
+        hot_o = jnp.where(row_n == (o & 127).astype(F32).astype(BF16), one, zero)
+        ct[i] = hot_c
+        ot[i] = hot_o
+        zr, xc = i // cx, i % cx
+        if 1 <= zr <= bz and 1 <= xc <= bx:
+            for dz in range(3):
+                for dx in range(3):
+                    col = xc - 1 + dx
+                    hot_rows[zr - 1, (dz * cx + col) * n : (dz * cx + col + 1) * n, (xc - 1) * n : xc * n] = (
+                        hot_o * (p == 3 * dz + dx).astype(F32).astype(BF16))
         at_c = dot(tab[a, b], hot_c)
         at_c = at_c[:8] + at_c[8:]
         around = jnp.concatenate(
@@ -194,116 +200,142 @@
         rows_live[i : i + 1] = part[6:7]
         rows_p[i : i + 1] = p
 
-    r = [geo[m] for m in range(3)]
-    dist = jnp.sqrt(r[0] * r[0] + r[1] * r[1] + r[2] * r[2] + SOFTEN)
-    inv = 1.0 / dist
-    q = dist / CUTOFF
-    rest = 1.0 - q * q
-    envelope = rest * rest
-    scale = inv * envelope
-    s1 = jnp.sin(math.pi * q)
-    c1 = jnp.cos(math.pi * q)
-    s0, c0, sk, ck = jnp.zeros_like(s1), jnp.ones_like(c1), s1, c1
-    for k in range(nb):
-        sins[k] = sk
-        coss[k] = ck
-        rad[k] = sk * scale
-        s0, sk = sk, 2.0 * c1 * sk - s0
-        c0, ck = ck, 2.0 * c1 * ck - c0
-    for m in range(3):
-        harm[m] = r[m] * inv
-    env_grad[...] = jnp.zeros_like(env_grad)
-    geo[3] = envelope
-
-    interior = {}
-    for i, (a, b) in enumerate(cells):
-        if bz <= a < 2 * bz and bx <= b < 2 * bx:
-            interior[i] = (a - bz) * bx + (b - bx)
-
-    group = 4 if total % 4 == 0 else 1
-    for g in range(0, total, group):
-        ids = list(range(g, g + group))
-        span = slice(g * n, (g + group) * n)
-        radial = join([rad[:, i, :] for i in ids], 1)
-        rh = rounded(radial)
-        x_s = xs[:, span]
-        parts = [rh, rh, radial - rh, x_s, x_s]
-        fill = kin - 3 * nb - 4 * spec
-        if fill:
-            parts.append(jnp.zeros((fill, group * n), F32))
-        pre = dot(in_t, jnp.concatenate(parts, axis=0).astype(BF16))
-        sig = 1.0 / (1.0 + jnp.exp(-pre))
-        latent = pre * sig
-        dsilu[:, span] = sig + latent * (1.0 - sig)
-        lh, ll = split(latent)
-        for t, i in enumerate(ids):
-            if i in interior:
-                l2[interior[i], 0] = lh[:, t * n : (t + 1) * n]
-                l2[interior[i], 1] = ll[:, t * n : (t + 1) * n]
-        alive = join([rows_live[i : i + 1] for i in ids], 1)
-        w = dot(env_t3, jnp.concatenate([lh, ll, lh], axis=0)) * alive
-        wts[:, span] = w
-        msgs = jnp.concatenate(
-            [w] + [w * join([harm[m, i : i + 1] for i in ids], 1) for m in range(3)], axis=0)
-        mh, ml = split(msgs)
-        for t, i in enumerate(ids):
-            cut = slice(t * n, (t + 1) * n)
-            hot_c = ct[i]
-            feat[:, i * n : (i + 1) * n] = dot_t(
-                jnp.concatenate([mh[:, cut], ml[:, cut]], axis=1),
-                jnp.concatenate([hot_c, hot_c], axis=1)).astype(BF16)
-
-    dfeat[...] = jnp.zeros_like(dfeat)
-    grad[...] = jnp.zeros_like(grad)
+    def geometry(c):
+        r = [geo[m, c] for m in range(3)]
+        dist = jnp.sqrt(r[0] * r[0] + r[1] * r[1] + r[2] * r[2] + SOFTEN)
+        inv = 1.0 / dist
+        q = dist / CUTOFF
+        rest = 1.0 - q * q
+        envelope = rest * rest
+        scale = inv * envelope
+        s1 = jnp.sin(math.pi * q)
+        c1 = jnp.cos(math.pi * q)
+        s0, c0, sk, ck = jnp.zeros_like(s1), jnp.ones_like(c1), s1, c1
+        for k in range(nb):
+            sins[k, c] = sk
+            coss[k, c] = ck
+            rad[k, c] = sk * scale
+            s0, sk = sk, 2.0 * c1 * sk - s0
+            c0, ck = ck, 2.0 * c1 * ck - c0
+        for m in range(3):
+            harm[m, c] = r[m] * inv
+        env_grad[c] = jnp.zeros_like(q)
+        geo[3, c] = envelope
+        geo[4, c] = inv
+        geo[5, c] = (-4.0 / CUTOFF) * q * rest
+
+    def latents(rows):
+        state = {}
+        for zr in rows:
+            ids = list(range(zr * cx, (zr + 1) * cx))
+            span = slice(zr * wide, (zr + 1) * wide)
+            radial = join([rad[:, i, :] for i in ids], 1)
+            rh = rounded(radial)
+            x_s = xs[:, span]
+            parts = [rh, rh, radial - rh, x_s, x_s]
+            fill = kin - 3 * nb - 4 * spec
+            if fill:
+                parts.append(jnp.zeros((fill, wide), F32))
+            pre = dot(in_t, jnp.concatenate(parts, axis=0).astype(BF16))
+            sig = 0.5 + 0.5 * jnp.tanh(0.5 * pre)
+            latent = pre * sig
+            dsilu[:, span] = sig + latent * (1.0 - sig)
+            lh, ll = split(latent)
+            if 1 <= zr <= bz:
+                l2[zr - 1, 0] = lh[:, n : n + inner]
+                l2[zr - 1, 1] = ll[:, n : n + inner]
+            alive = join([rows_live[i : i + 1] for i in ids], 1)
+            w = dot(env_t3, jnp.concatenate([lh, ll, lh], axis=0)) * alive
+            wts[:, span] = w
+            msgs = jnp.concatenate(
+                [w] + [w * join([harm[m, i : i + 1] for i in ids], 1) for m in range(3)], axis=0)
+            mh, ml = split(msgs)
+            for t, i in enumerate(ids):
+                cut = slice(t * n, (t + 1) * n)
+                hot_c = ct[i]
+                feat[:, i * n : (i + 1) * n] = dot_t(
+                    jnp.concatenate([mh[:, cut], ml[:, cut]], axis=1),
+                    jnp.concatenate([hot_c, hot_c], axis=1)).astype(BF16)
+
+    early = [zr for zr in range(cz) if zr >= 2]
+    late = [zr for zr in range(cz) if zr < 2]
+
+    for copy, key in zip(first, [key for key, _ in others_list]):
+        if key[0] != (-1) % nz:
+            copy.wait()
+    tables(range(bz, 2 * bz + 2))
+    for i in range(2 * cx, cz * cx):
+        gather(i)
+    geometry(slice(2 * cx, cz * cx))
+    latents(early)
+    for copy, key in zip(first, [key for key, _ in others_list]):
+        if key[0] == (-1) % nz:
+            copy.wait()
+    tables(range(bz - 2, bz))
+    for i in range(2 * cx):
+        gather(i)
+    geometry(slice(0, 2 * cx))
+    latents(late)
+
     row_8 = lax.broadcasted_iota(jnp.int32, (16, n), 0)
-    for i, k in interior.items():
-        hot_c, hot_o = ct[i], ot[i]
-        p = rows_p[i : i + 1]
-        env_row = geo[3, i : i + 1]
-        alive = rows_live[i : i + 1]
-        f_c = dot(feat[:, i * n : (i + 1) * n], hot_c)
-        f_o = None
-        hots = []
-        for dz in range(3):
-            start = i + (dz - 1) * cx - 1
-            hot3 = jnp.concatenate(
-                [hot_o * (p == 3 * dz + dx).astype(F32).astype(BF16) for dx in range(3)], axis=0)
-            hots.append((start, hot3))
-            term = dot(feat[:, start * n : (start + 3) * n], hot3)
-            f_o = term if f_o is None else f_o + term
-        prod4 = f_c * f_o
+    out_rows = jnp.concatenate([out_col] * bx, axis=1)
+    inner_rows = range(1, bz + 1)
+
+    def ids_of(zr):
+        return [zr * cx + b for b in range(1, bx + 1)]
+
+    f_cs, f_os = {}, {}
+    for zr in inner_rows:
+        f_cs[zr] = join([dot(feat[:, i * n : (i + 1) * n], ct[i]) for i in ids_of(zr)], 1)
+        f_os[zr] = dot(feat[:, (zr - 1) * wide : (zr + 2) * wide], hot_rows[zr - 1])
+    us = {}
+    for zr in inner_rows:
+        prod4 = f_cs[zr] * f_os[zr]
         prod = prod4[:ch] + prod4[ch : 2 * ch] + prod4[2 * ch : 3 * ch] + prod4[3 * ch :]
         ph, pl_ = split(prod)
-        parts = [l2[k, 0], l2[k, 1], l2[k, 0], ph, pl_, ph]
+        parts = [l2[zr - 1, 0], l2[zr - 1, 1], l2[zr - 1, 0], ph, pl_, ph]
         if kpad:
-            parts.append(jnp.zeros((kpad, n), BF16))
-        u = dot(up_t, jnp.concatenate(parts, axis=0))
-        sig = 1.0 / (1.0 + jnp.exp(-u))
+            parts.append(jnp.zeros((kpad, inner), BF16))
+        us[zr] = dot(up_t, jnp.concatenate(parts, axis=0))
+    joins, raws = {}, {}
+    for zr in inner_rows:
+        env_row = join([geo[3, i : i + 1] for i in ids_of(zr)], 1)
+        alive = join([rows_live[i : i + 1] for i in ids_of(zr)], 1)
+        u = us[zr]
+        sig = 0.5 + 0.5 * jnp.tanh(0.5 * u)
         hid = u * sig
-        raw = jnp.sum(out_col * hid, axis=0, keepdims=True) * alive
-        env_grad[i : i + 1] = raw
-        e_row = raw * env_row
-        e_hi = rounded(e_row)
-        e_rows = jnp.where(row_8 == 0, e_hi, jnp.where(row_8 == 1, e_row - e_hi, 0.0)).astype(BF16)
-        e_atom = dot_t(e_rows, hot_c)
-        grad[0, k // bx, k % bx, 3:4] = -(e_atom[0:1] + e_atom[1:2])
-        d_u = out_col * (alive * env_row) * (sig + hid * (1.0 - sig))
+        raws[zr] = jnp.sum(out_rows * hid, axis=0, keepdims=True) * alive
+        d_u = out_rows * (alive * env_row) * (sig + hid * (1.0 - sig))
         dh, dl = split(d_u)
-        d_join = dot(up3, jnp.concatenate([dh, dl, dh], axis=0))
-        dlat_own[k] = d_join[:lat]
+        joins[zr] = dot(up3, jnp.concatenate([dh, dl, dh], axis=0))
+    for zr in inner_rows:
+        d_join = joins[zr]
+        dlat_own[zr - 1] = d_join[:lat]
         d_prod = jnp.concatenate([d_join[lat:]] * 4, axis=0)
-        dch, dcl = split(d_prod * f_o)
-        doh, dol = split(d_prod * f_c)
-        dfeat[:, i * n : (i + 1) * n] += dot_t(
-            jnp.concatenate([dch, dcl], axis=1), jnp.concatenate([hot_c, hot_c], axis=1))
-        d_o = jnp.concatenate([doh, dol], axis=1)
-        for start, hot3 in hots:
-            dfeat[:, start * n : (start + 3) * n] += dot_t(
-                d_o, jnp.concatenate([hot3, hot3], axis=1))
-
-    for g in range(0, total, group):
-        ids = list(range(g, g + group))
-        span = slice(g * n, (g + group) * n)
+        dc = (d_prod * f_os[zr]).astype(BF16)
+        do = (d_prod * f_cs[zr]).astype(BF16)
+        part = dot_t(do, hot_rows[zr - 1])
+        if zr == 1:
+            dfeat[:, : 3 * wide] = part
+            if cz > 3:
+                dfeat[:, 3 * wide :] = jnp.zeros((4 * ch, (cz - 3) * wide), F32)
+        else:
+            dfeat[:, (zr - 1) * wide : (zr + 2) * wide] += part
+        for t, i in enumerate(ids_of(zr)):
+            dfeat[:, i * n : (i + 1) * n] += dot_t(dc[:, t * n : (t + 1) * n], ct[i])
+    for zr in inner_rows:
+        for t, i in enumerate(ids_of(zr)):
+            raw = raws[zr][:, t * n : (t + 1) * n]
+            env_grad[i : i + 1] = raw
+            e_row = raw * geo[3, i : i + 1]
+            e_hi = rounded(e_row)
+            e_rows = jnp.where(row_8 == 0, e_hi, jnp.where(row_8 == 1, e_row - e_hi, 0.0)).astype(BF16)
+            e_atom = dot_t(e_rows, ct[i])
+            grad[0, zr - 1, t, 3:4] = -(e_atom[0:1] + e_atom[1:2])
+
+    for zr in range(cz):
+        ids = list(range(zr * cx, (zr + 1) * cx))
+        span = slice(zr * wide, (zr + 1) * wide)
         dm = []
         for i in ids:
             hot_c = ct[i]
@@ -322,11 +354,11 @@
         wh, wl = split(dw)
         parts = [wh, wl, wh]
         if kpad:
-            parts.append(jnp.zeros((kpad, group * n), BF16))
+            parts.append(jnp.zeros((kpad, wide), BF16))
         d_lat = dot(env3, jnp.concatenate(parts, axis=0))
-        if any(i in interior for i in ids):
-            d_lat = d_lat + join(
-                [dlat_own[interior[i]] if i in interior else jnp.zeros((lat, n), F32) for i in ids], 1)
+        if 1 <= zr <= bz:
+            side = jnp.zeros((lat, n), F32)
+            d_lat = d_lat + jnp.concatenate([side, dlat_own[zr - 1], side], axis=1)
         dh, dl = split(d_lat * dsilu[:, span])
         d_r = dot(wr3, jnp.concatenate([dh, dl, dh], axis=0))
         for t, i in enumerate(ids):
@@ -337,7 +369,9 @@
     for k in range(1, nb):
         sum_s = sum_s + drad[k] * sins[k]
         sum_c = sum_c + (k + 1.0) * (drad[k] * coss[k])
-    env_slope = (-4.0 / CUTOFF) * q * rest
+    r = [geo[m] for m in range(3)]
+    inv, env_slope = geo[4], geo[5]
+    scale = inv * geo[3]
     d_dist = (
         (math.pi / CUTOFF) * sum_c * scale
         - sum_s * scale * inv
@@ -413,20 +447,21 @@
             vmem((3 * bz, 3 * bx, 16, n), BF16),
             vmem((cells, n, n), BF16),
             vmem((cells, n, n), BF16),
+            vmem((bz, 3 * (bx + 2) * n, bx * n), BF16),
             vmem((cells, n)),
             vmem((cells, n), jnp.int32),
-            vmem((4, cells, n)),
+            vmem((6, cells, n)),
             vmem((2 * spec, cells * n)),
             vmem((nb, cells, n)),
             vmem((nb, cells, n)),
             vmem((nb, cells, n)),
             vmem((3, cells, n)),
-            vmem((bz * bx, 2, lat, n), BF16),
+            vmem((bz, 2, lat, bx * n), BF16),
             vmem((lat, cells * n)),
             vmem((ch, cells * n)),
             vmem((4 * ch, cells * n), BF16),
             vmem((4 * ch, cells * n)),
-            vmem((bz * bx, lat, n)),
+            vmem((bz, lat, bx * n)),
             vmem((cells, n)),
             vmem((3, cells, n)),
             vmem((nb, cells, n)),

time: 22.3 us -> 20.9 us (0.937)
  Pallas kernels: 20.3 us -> 18.9 us
    pallas_call x1, Pallas kernels: 20.3 us -> 18.9 us  [body(): pl.pallas_call(functools.partial(kernel, nz, nx, bz, bx, nb, spec, ch, la...]
where the time goes in v2:
time: 20.9 us; the launch traced here: 20.7 us
  Pallas kernels  18.9 us (90%)
  local copies, waits for them, and re-layouts  1.17 us (6%)
  between operations  0.64 us (3%)
    pallas_call x1, Pallas kernels, body(): pl.pallas_call(functools.partial(kernel, nz, nx, bz, bx, nb, spec, ch, la...  18.9 us
    slice x1, local copies, waits for them, and re-layouts, body(): return (result[3], result[:3])  0.59 us
    squeeze x1, local copies, waits for them, and re-layouts, body(): return (result[3], result[:3])  0.58 us

profile of v2, /device:TPU:0, one launch (start us, length us, event | category | flops | bytes accessed | tf_op | source)
XLA Modules:
  0.0 20.7 jit_solution(16199115691744825080)
XLA Ops:
  0.6 18.9 %shard_map.104 = f32[4,2,2,128]{3,2,1,0:T(2,128)S(1)} custom-call(f32[3,2,2,128]{3,2,1,0:T(2,128)} %coords_hbm.1, s32[2,2,128]{2,1,0:T(2,128)} %species_hbm.1, s32[2,2,128]{2,1,0:T(2,128)} %centers_hbm.1, s32[2,2,128]{2,1,0:T(2,128)} %others_hbm.1, s32[2,2]{1,0:T(2,128)} %live_hbm.1, f32[24,128]{1,0:T(8,128)} %in_hbm.1, f32[32,128]{1,0:T(8,128)} %bitcast.4, ...), custom_call_target="tpu_custom_call" | custom-call | tf_op jit(solution)/shard_map/pallas_call | solution.py:474
  19.5 0.6 %slice_bitcast_fusion = f32[2,2,128]{2,1,0:T(2,128)} fusion(f32[4,2,2,128]{3,2,1,0:T(2,128)S(1)} %shard_map.104), kind=kLoop, calls=%fused_computation | loop fusion | bytes 4096 | tf_op jit(solution)/shard_map/squeeze | solution.py:482
  20.1 0.6 %slice.7 = f32[3,2,2,128]{3,2,1,0:T(2,128)} slice(f32[4,2,2,128]{3,2,1,0:T(2,128)S(1)} %shard_map.104), slice={[0:3], [0:2], [0:2], [0:128]} | slice | bytes 12288 | tf_op jit(solution)/shard_map/slice | solution.py:482

commit v3 on v2

v3 whole, which is shorter than its diff:
```python
import functools
import math

import jax
import jax.numpy as jnp
from jax import lax
from jax.experimental import pallas as pl
from jax.experimental.pallas import tpu as pltpu
from jax.sharding import PartitionSpec as P

SOFTEN = 0.01
CUTOFF = 3.5
F32 = jnp.float32
BF16 = jnp.bfloat16
MESH = pl.DeviceIdType.MESH


def rounded(x):
    return x.astype(BF16).astype(F32)


def split(x):
    high = x.astype(BF16)
    return high, (x - high.astype(F32)).astype(BF16)


def dot(a, b):
    return jnp.dot(a, b, preferred_element_type=F32)


def dot_t(a, b):
    return lax.dot_general(a, b, (((1,), (1,)), ((), ())), preferred_element_type=F32)


def join(parts, axis):
    return parts[0] if len(parts) == 1 else jnp.concatenate(parts, axis=axis)


def neighbours(nz, nx):
    slots = {(0, 0): 0}
    for dz in (-1, 0, 1):
        for dx in (-1, 0, 1):
            slots.setdefault((dz % nz, dx % nx), len(slots))
    return slots


def kernel(
    nz, nx, bz, bx, nb, spec, ch, lat,
    coords_hbm, species_hbm, centers_hbm, others_hbm, live_hbm, in_hbm, env_hbm, up_hbm, out_hbm,
    result_ref,
    coords_ref, species_ref, centers_ref, others_ref, live_ref, in_ref, env_ref, up_ref, out_ref,
    atoms, edges, tab, hot, hot_t, rows_hot, rows_hot_t, codes, rows_c, rows_o, rows_p, rows_live,
    diffs, geo, xs, sins, coss, rad, harm,
    l2, dsilu, wts, feat, dfeat, dlat_own, env_grad, dharm, drad, gr, grad, give_ref, back,
    send1, recv1, send2, recv2, send3, recv3, load_sem,
):
    n = coords_ref.shape[-1]
    slots = neighbours(nz, nx)
    me_z, me_x = lax.axis_index("gz"), lax.axis_index("xy")
    mine = slots[(1 % nz, 0)]
    others_list = [(key, s) for key, s in slots.items() if s != mine]
    index = {s: i for i, (_, s) in enumerate(others_list)}

    def owner(key):
        return (lax.rem(me_z + (key[0] - 1) % nz, nz), lax.rem(me_x + key[1], nx))

    def user(key):
        return (lax.rem(me_z + (1 - key[0]) % nz, nz), lax.rem(me_x + (-key[1]) % nx, nx))

    barrier = pltpu.get_barrier_semaphore()
    for key, _ in others_list:
        pl.semaphore_signal(barrier, inc=1, device_id=owner(key), device_id_type=MESH)

    loads = [
        pltpu.make_async_copy(source, target, load_sem.at[k])
        for k, (source, target) in enumerate([
            (coords_hbm, coords_ref), (species_hbm, species_ref), (centers_hbm, centers_ref),
            (others_hbm, others_ref), (live_hbm, live_ref), (in_hbm, in_ref), (env_hbm, env_ref),
            (up_hbm, up_ref), (out_hbm, out_ref)])
    ]
    for load in loads:
        load.start()
    for load in loads[:5]:
        load.wait()
    lane = lax.broadcasted_iota(jnp.int32, (1, n), 1)
    for a in range(bz):
        for b in range(bx):
            code = centers_ref[a, b : b + 1, :] + 128 * others_ref[a, b : b + 1, :]
            code = jnp.where(lane < live_ref[a : a + 1, b : b + 1], code, -1)
            edges[mine, a, b : b + 1, :] = code.astype(F32)
            atoms[mine, a, b] = jnp.concatenate(
                [coords_ref[:, a, b, :], species_ref[a, b : b + 1, :].astype(F32)], axis=0)
    pl.semaphore_wait(barrier, len(others_list))
    first = {}
    for key, s in others_list:
        i = index[s]
        for ref, send, recv in ((atoms, send1, recv1), (edges, send3, recv3)):
            copy = pltpu.make_async_remote_copy(
                src_ref=ref.at[mine], dst_ref=ref.at[s], send_sem=send.at[i],
                recv_sem=recv.at[i], device_id=user(key), device_id_type=MESH,
            )
            copy.start()
            first.setdefault(key, []).append(copy)

    for load in loads[5:]:
        load.wait()
    w_in = in_ref[...]
    w_hi = rounded(w_in)
    w_lo = w_in - w_hi
    gap = jnp.zeros((nb, lat), F32)
    kin = 4 * nb + 4 * spec
    w_rows = [w_hi[:nb], w_hi[:nb], w_lo[:nb], gap, w_hi[nb:], w_lo[nb:]]
    if lat > kin:
        w_rows.append(jnp.zeros((lat - kin, lat), F32))
    in_t = jnp.concatenate(w_rows, axis=0).T.astype(BF16)[:, :kin]
    wr2 = jnp.concatenate(
        [jnp.concatenate([w_hi[:nb], w_hi[:nb]], axis=1), jnp.concatenate([w_lo[:nb], gap], axis=1)],
        axis=0).astype(BF16)
    env_t = env_ref[...]
    et_hi = rounded(env_t)
    et_lo = env_t - et_hi
    env_t2 = jnp.concatenate(
        [jnp.concatenate([et_hi, et_hi], axis=1), jnp.concatenate([et_lo, jnp.zeros_like(et_lo)], axis=1)],
        axis=0).astype(BF16)
    kpad = -(3 * ch) % lat
    env3 = jnp.concatenate(
        [et_hi, et_hi, et_lo] + ([jnp.zeros((kpad, lat), F32)] if kpad else []), axis=0
    ).T.astype(BF16)
    up = up_ref[...]
    up_hi = rounded(up)
    up_lo = up - up_hi
    up3 = jnp.concatenate([up_hi, up_hi, up_lo], axis=1).astype(BF16)
    up_t = jnp.concatenate(
        [x.T.astype(BF16) for x in (up_hi[:lat], up_hi[:lat], up_lo[:lat])]
        + [jnp.concatenate(
            [up_hi[lat:], up_hi[lat:], up_lo[lat:]]
            + ([jnp.zeros((kpad, lat), F32)] if kpad else []), axis=0).T.astype(BF16)],
        axis=1)
    out_col = jnp.broadcast_to(out_ref[...], (n, lat)).T

    rows_hot[...] = jnp.zeros_like(rows_hot)
    rows_hot_t[...] = jnp.zeros_like(rows_hot_t)
    grad[...] = jnp.zeros_like(grad)
    cz, cx = bz + 2, bx + 2
    total = cz * cx
    wide = cx * n
    inner = bx * n
    cells = [(a, b) for a in range(bz - 1, 2 * bz + 1) for b in range(bx - 1, 2 * bx + 1)]
    row_n = lax.broadcasted_iota(jnp.int32, (n, n), 0).astype(F32).astype(BF16)
    row_s = lax.broadcasted_iota(jnp.int32, (spec, n), 0).astype(F32)
    one, zero = jnp.ones((n, n), BF16), jnp.zeros((n, n), BF16)

    def place(a, b):
        return slots[((a // bz - 1) % nz, (b // bx - 1) % nx)], a % bz, b % bx

    def tables(rows):
        for a in rows:
            hl = {}
            for b in range(bx - 2, 2 * bx + 2):
                s, i, j = place(a, b)
                part = atoms[s, i, j]
                hi = rounded(part)
                hl[b] = jnp.concatenate([hi, part - hi], axis=0)
            for b in range(bx - 1, 2 * bx + 1):
                tab[a, b] = jnp.concatenate(
                    [hl[b - 1], hl[b], hl[b + 1], jnp.zeros((8, n), F32)], axis=0).astype(BF16)

    def decode(rows):
        c = slice(rows[0] * cx, (rows[-1] + 1) * cx)
        for i in range(rows[0] * cx, (rows[-1] + 1) * cx):
            s, y, x = place(*cells[i])
            codes[i : i + 1] = edges[s, y, x : x + 1, :]
        code = codes[c].astype(jnp.int32)
        o = code >> 7
        rows_c[c] = (code & 127).astype(F32)
        rows_o[c] = (o & 127).astype(F32)
        rows_p[c] = o >> 7
        rows_live[c] = (code >= 0).astype(F32)

    def gather(i):
        a, b = cells[i]
        p = rows_p[i : i + 1]
        hot_c = jnp.where(row_n == rows_c[i : i + 1].astype(BF16), one, zero)
        hot_o = jnp.where(row_n == rows_o[i : i + 1].astype(BF16), one, zero)
        both = jnp.concatenate([hot_c, hot_o], axis=1)
        hot[i] = both
        hot_t[i] = jnp.concatenate([hot_c.T, hot_o.T], axis=1)
        zr, xc = i // cx, i % cx
        if 1 <= zr <= bz and 1 <= xc <= bx:
            for dz in range(3):
                for dx in range(3):
                    col = dz * cx + xc - 1 + dx
                    masked = hot_o * (p == 3 * dz + dx).astype(F32).astype(BF16)
                    rows_hot[zr - 1, col * n : (col + 1) * n, (xc - 1) * n : xc * n] = masked
                    rows_hot_t[zr - 1, (xc - 1) * n : xc * n, col * n : (col + 1) * n] = masked.T
        around = jnp.concatenate([tab[a + dz, b] for dz in (-1, 0, 1)], axis=0)
        got = dot(around, both)
        at_c = got[40:48, :n]
        at_o = jnp.zeros((8, n), F32)
        for dz in range(3):
            for dx in range(3):
                at_o = jnp.where(p == 3 * dz + dx, got[32 * dz + 8 * dx : 32 * dz + 8 * dx + 8, n:], at_o)
        at_c = at_c[:4] + at_c[4:]
        at_o = at_o[:4] + at_o[4:]
        diffs[i] = at_o - at_c
        xs[:, i * n : (i + 1) * n] = jnp.concatenate(
            [(row_s == at_c[3:4]).astype(F32), (row_s == at_o[3:4]).astype(F32)], axis=0).astype(BF16)

    def geometry(rows):
        c = slice(rows[0] * cx, (rows[-1] + 1) * cx)
        p = rows_p[c]
        third = (p >= 3).astype(jnp.int32) + (p >= 6).astype(jnp.int32)
        r = [
            diffs[c, 0, :] + (third - 1).astype(F32),
            diffs[c, 1, :] + (p - 3 * third - 1).astype(F32),
            diffs[c, 2, :],
        ]
        dist = jnp.sqrt(r[0] * r[0] + r[1] * r[1] + r[2] * r[2] + SOFTEN)
        inv = 1.0 / dist
        q = dist / CUTOFF
        rest = 1.0 - q * q
        envelope = rest * rest
        scale = inv * envelope
        s1 = jnp.sin(math.pi * q)
        c1 = jnp.cos(math.pi * q)
        s0, c0, sk, ck = jnp.zeros_like(s1), jnp.ones_like(c1), s1, c1
        for k in range(nb):
            sins[k, c] = sk
            coss[k, c] = ck
            rad[k, c] = sk * scale
            s0, sk = sk, 2.0 * c1 * sk - s0
            c0, ck = ck, 2.0 * c1 * ck - c0
        for m in range(3):
            harm[m, c] = r[m] * inv
            geo[m, c] = r[m]
        env_grad[c] = jnp.zeros_like(q)
        geo[3, c] = envelope
        geo[4, c] = inv
        geo[5, c] = (-4.0 / CUTOFF) * q * rest

    def ids_of(zr):
        return list(range(zr * cx, (zr + 1) * cx))

    def inner_of(zr):
        return ids_of(zr)[1:-1]

    def latents(rows):
        pres, lows, mls = {}, {}, {}
        for zr in rows:
            span = slice(zr * wide, (zr + 1) * wide)
            radial = join([rad[:, i, :] for i in ids_of(zr)], 1)
            rh = rounded(radial)
            x_s = xs[:, span]
            pres[zr] = dot(in_t, jnp.concatenate([
                jnp.concatenate([rh, radial - rh], axis=0).astype(BF16),
                jnp.concatenate([rh, jnp.zeros_like(rh)], axis=0).astype(BF16), x_s, x_s], axis=0))
        for zr in rows:
            span = slice(zr * wide, (zr + 1) * wide)
            pre = pres[zr]
            sig = 0.5 + 0.5 * jnp.tanh(0.5 * pre)
            latent = pre * sig
            dsilu[:, span] = sig + latent * (1.0 - sig)
            lh, ll = split(latent)
            if 1 <= zr <= bz:
                l2[zr - 1, 0] = lh[:, n : n + inner]
                l2[zr - 1, 1] = ll[:, n : n + inner]
            lows[zr] = dot(env_t2, jnp.concatenate([lh, ll], axis=0))
        for zr in rows:
            span = slice(zr * wide, (zr + 1) * wide)
            ids = ids_of(zr)
            w = lows[zr]
            w = (w[:ch] + w[ch:]) * join([rows_live[i : i + 1] for i in ids], 1)
            wts[:, span] = w
            msgs = jnp.concatenate(
                [w] + [w * join([harm[m, i : i + 1] for i in ids], 1) for m in range(3)], axis=0)
            mls[zr] = split(msgs)
            mh, ml = mls[zr]
            for t, i in enumerate(ids):
                cut = slice(t * n, (t + 1) * n)
                hot_c = hot_t[i, :, :n]
                feat[:, i * n : (i + 1) * n] = dot(
                    jnp.concatenate([mh[:, cut], ml[:, cut]], axis=1),
                    jnp.concatenate([hot_c, hot_c], axis=0)).astype(BF16)

    early, late = list(range(2, cz)), [0, 1]
    for copies in first.values():
        for copy in copies:
            copy.wait()
    every = list(range(cz))
    decode(every)
    tables(range(bz - 2, 2 * bz + 2))
    for i in range(total):
        gather(i)
    geometry(every)
    latents(every)

    row_16 = lax.broadcasted_iota(jnp.int32, (16, n), 0)
    out_rows = jnp.concatenate([out_col] * bx, axis=1)
    inner_rows = range(1, bz + 1)
    f_cs, f_os, us, joins, raws = {}, {}, {}, {}, {}
    for zr in inner_rows:
        f_cs[zr] = join([dot(feat[:, i * n : (i + 1) * n], hot[i, :, :n]) for i in inner_of(zr)], 1)
        f_os[zr] = dot(feat[:, (zr - 1) * wide : (zr + 2) * wide], rows_hot[zr - 1])
    for zr in inner_rows:
        prod4 = f_cs[zr] * f_os[zr]
        prod = prod4[:ch] + prod4[ch : 2 * ch] + prod4[2 * ch : 3 * ch] + prod4[3 * ch :]
        ph, pl_ = split(prod)
        parts = [l2[zr - 1, 0], l2[zr - 1, 1], l2[zr - 1, 0], ph, pl_, ph]
        if kpad:
            parts.append(jnp.zeros((kpad, inner), BF16))
        us[zr] = dot(up_t, jnp.concatenate(parts, axis=0))
    for zr in inner_rows:
        env_row = join([geo[3, i : i + 1] for i in inner_of(zr)], 1)
        alive = join([rows_live[i : i + 1] for i in inner_of(zr)], 1)
        u = us[zr]
        sig = 0.5 + 0.5 * jnp.tanh(0.5 * u)
        hid = u * sig
        raws[zr] = jnp.sum(out_rows * hid, axis=0, keepdims=True) * alive
        d_u = out_rows * (alive * env_row) * (sig + hid * (1.0 - sig))
        dh, dl = split(d_u)
        joins[zr] = dot(up3, jnp.concatenate([dh, dl, dh], axis=0))
    for zr in inner_rows:
        d_join = joins[zr]
        dlat_own[zr - 1] = d_join[:lat]
        d_prod = jnp.concatenate([d_join[lat:]] * 4, axis=0)
        dch, dcl = split(d_prod * f_os[zr])
        doh, dol = split(d_prod * f_cs[zr])
        turned_rows = rows_hot_t[zr - 1]
        part = dot(jnp.concatenate([doh, dol], axis=1), jnp.concatenate([turned_rows, turned_rows], axis=0))
        if zr == 1:
            dfeat[:, : 3 * wide] = part
            if cz > 3:
                dfeat[:, 3 * wide :] = jnp.zeros((4 * ch, (cz - 3) * wide), F32)
        else:
            dfeat[:, (zr - 1) * wide : (zr + 2) * wide] += part
        for t, i in enumerate(inner_of(zr)):
            raw = raws[zr][:, t * n : (t + 1) * n]
            env_grad[i : i + 1] = raw
            e_row = raw * geo[3, i : i + 1]
            e_hi = rounded(e_row)
            e_lo = jnp.where(row_16 == 0, e_row - e_hi, 0.0).astype(BF16)
            e_hi = jnp.where(row_16 == 0, e_hi, 0.0).astype(BF16)
            cut = slice(t * n, (t + 1) * n)
            hot_c = hot_t[i, :, :n]
            both = dot(
                jnp.concatenate([
                    jnp.concatenate([dch[:, cut], e_hi], axis=0),
                    jnp.concatenate([dcl[:, cut], e_lo], axis=0)], axis=1),
                jnp.concatenate([hot_c, hot_c], axis=0))
            dfeat[:, i * n : (i + 1) * n] += both[: 4 * ch]
            grad[0, zr - 1, t, 3:4] = -both[4 * ch : 4 * ch + 1]

    def backward(rows):
        dms, dls = {}, {}
        for zr in rows:
            dm = []
            for i in ids_of(zr):
                hot_c = hot[i, :, :n]
                fh, fl = split(dfeat[:, i * n : (i + 1) * n])
                dm.append(dot(jnp.concatenate([fh, fl], axis=1), jnp.concatenate([hot_c, hot_c], axis=0)))
            dms[zr] = join(dm, 1)
        for zr in rows:
            ids = ids_of(zr)
            dm = dms[zr]
            dw = dm[:ch]
            for m in range(3):
                dw = dw + dm[(m + 1) * ch : (m + 2) * ch] * join([harm[m, i : i + 1] for i in ids], 1)
            dw = dw * join([rows_live[i : i + 1] for i in ids], 1)
            wh, wl = split(dw)
            parts = [wh, wl, wh]
            if kpad:
                parts.append(jnp.zeros((kpad, wide), BF16))
            dls[zr] = dot(env3, jnp.concatenate(parts, axis=0))
        for zr in rows:
            span = slice(zr * wide, (zr + 1) * wide)
            d_lat = dls[zr]
            if 1 <= zr <= bz:
                side = jnp.zeros((lat, n), F32)
                d_lat = d_lat + jnp.concatenate([side, dlat_own[zr - 1], side], axis=1)
            dh, dl = split(d_lat * dsilu[:, span])
            d_r = dot(wr2, jnp.concatenate([dh, dl], axis=0))
            d_r = d_r[:nb] + d_r[nb:]
            for t, i in enumerate(ids_of(zr)):
                drad[:, i, :] = d_r[:, t * n : (t + 1) * n]
        for zr in rows:
            span = slice(zr * wide, (zr + 1) * wide)
            w = wts[:, span]
            for m in range(3):
                d_h = jnp.sum(dms[zr][(m + 1) * ch : (m + 2) * ch] * w, axis=0, keepdims=True)
                for t, i in enumerate(ids_of(zr)):
                    dharm[m, i : i + 1] = d_h[:, t * n : (t + 1) * n]

    def radial_backward(rows):
        c = slice(rows[0] * cx, (rows[-1] + 1) * cx)
        sum_s = drad[0, c] * sins[0, c]
        sum_c = drad[0, c] * coss[0, c]
        for k in range(1, nb):
            sum_s = sum_s + drad[k, c] * sins[k, c]
            sum_c = sum_c + (k + 1.0) * (drad[k, c] * coss[k, c])
        inv, env_slope = geo[4, c], geo[5, c]
        scale = inv * geo[3, c]
        d_dist = (
            (math.pi / CUTOFF) * sum_c * scale
            - sum_s * scale * inv
            + (sum_s * inv + env_grad[c]) * env_slope
        )
        for m in range(3):
            d_dist = d_dist - dharm[m, c] * geo[m, c] * (inv * inv)
        for m in range(3):
            d_m = d_dist * harm[m, c] + dharm[m, c] * inv
            hi = rounded(d_m)
            gr[c, m, :] = hi
            gr[c, m + 4, :] = d_m - hi
        gr[c, 3, :] = jnp.zeros_like(inv)
        gr[c, 7, :] = jnp.zeros_like(inv)

    def scatter(i):
        a, b = cells[i]
        g8 = gr[i]
        p = rows_p[i : i + 1]
        stack = [g8] + [jnp.where(p == off, g8, 0.0) for off in range(9)]
        out = dot(jnp.concatenate(stack, axis=0).astype(BF16), hot_t[i])
        s, y, x = place(a, b)
        grad[s, y, x] -= out[:8, :n]
        for off in range(9):
            s, y, x = place(a + off // 3 - 1, b + off % 3 - 1)
            grad[s, y, x] += out[8 + 8 * off : 16 + 8 * off, n:]

    second = {}

    def give(later):
        for key, s in others_list:
            if s in second or s in later:
                continue
            i = index[s]
            for y in range(bz):
                for x in range(bx):
                    acc = grad[s, y, x]
                    give_ref[i, y, x] = acc[:4] + acc[4:]
            second[s] = pltpu.make_async_remote_copy(
                src_ref=give_ref.at[i], dst_ref=back.at[i], send_sem=send2.at[i],
                recv_sem=recv2.at[i], device_id=owner(key), device_id_type=MESH,
            )
            second[s].start()

    def targets(rows):
        return {
            place(cells[i][0] + dz, cells[i][1] + dx)[0]
            for zr in rows for i in ids_of(zr) for dz in (-1, 0, 1) for dx in (-1, 0, 1)}

    backward(early[::-1])
    radial_backward(early)
    for zr in reversed(early):
        for i in ids_of(zr):
            scatter(i)
    give(targets(late))
    backward(late[::-1])
    radial_backward(late)
    for zr in reversed(late):
        for i in ids_of(zr):
            scatter(i)
    give(set())
    for copy in second.values():
        copy.wait()
    for a in range(bz):
        for b in range(bx):
            acc = grad[mine, a, b]
            acc = acc[:4] + acc[4:]
            for s in range(len(others_list)):
                acc = acc + back[s, a, b]
            result_ref[:, a, b, :] = -acc


def deliver(result_ref, energy_ref, force_ref, sem):
    copies = [
        pltpu.make_async_copy(result_ref.at[3], energy_ref, sem.at[0]),
        pltpu.make_async_copy(result_ref.at[pl.ds(0, 3)], force_ref, sem.at[1]),
    ]
    for copy in copies:
        copy.start()
    for copy in copies:
        copy.wait()


def solution(mesh):
    nz, nx = mesh.shape["gz"], mesh.shape["xy"]

    def body(coords, species, centers, others, live_count, in_weight, env_weight, up_weight, out_weight):
        _, bz, bx, n = coords.shape
        lat, ch = env_weight.shape
        nb = 8
        spec = (in_weight.shape[0] - nb) // 2
        cells = (bz + 2) * (bx + 2)
        ns = len(neighbours(nz, nx)) - 1
        vmem = lambda shape, dtype=F32: pltpu.VMEM(shape, dtype)
        args = (coords, species, centers, others, live_count, in_weight, env_weight.T, up_weight,
                out_weight[None])
        scratch = [vmem(x.shape, x.dtype) for x in args] + [
            vmem((ns + 1, bz, bx, 4, n)),
            vmem((ns + 1, bz, bx, n)),
            vmem((3 * bz, 3 * bx, 32, n), BF16),
            vmem((cells, n, 2 * n), BF16),
            vmem((cells, n, 2 * n), BF16),
            vmem((bz, 3 * (bx + 2) * n, bx * n), BF16),
            vmem((bz, bx * n, 3 * (bx + 2) * n), BF16),
            vmem((cells, n)),
            vmem((cells, n)),
            vmem((cells, n)),
            vmem((cells, n), jnp.int32),
            vmem((cells, n)),
            vmem((cells, 4, n)),
            vmem((6, cells, n)),
            vmem((2 * spec, cells * n), BF16),
            vmem((nb, cells, n)),
            vmem((nb, cells, n)),
            vmem((nb, cells, n)),
            vmem((3, cells, n)),
            vmem((bz, 2, lat, bx * n), BF16),
            vmem((lat, cells * n)),
            vmem((ch, cells * n)),
            vmem((4 * ch, cells * n), BF16),
            vmem((4 * ch, cells * n)),
            vmem((bz, lat, bx * n)),
            vmem((cells, n)),
            vmem((3, cells, n)),
            vmem((nb, cells, n)),
            vmem((cells, 8, n)),
            vmem((ns + 1, bz, bx, 8, n)),
            vmem((ns, bz, bx, 4, n)),
            vmem((ns, bz, bx, 4, n)),
        ] + [pltpu.SemaphoreType.DMA((ns,)) for _ in range(6)]
        scratch.append(pltpu.SemaphoreType.DMA((len(args),)))
        specs = [pl.BlockSpec(memory_space=pl.ANY) for _ in args]
        result = pl.pallas_call(
            functools.partial(kernel, nz, nx, bz, bx, nb, spec, ch, lat),
            out_shape=pltpu.VMEM((4, bz, bx, n), F32),
            in_specs=specs,
            out_specs=pl.BlockSpec(memory_space=pltpu.VMEM),
            scratch_shapes=scratch,
            compiler_params=pltpu.CompilerParams(collective_id=0, has_side_effects=True),
        )(*args)
        return pl.pallas_call(
            deliver,
            out_shape=(jax.ShapeDtypeStruct((bz, bx, n), F32), jax.ShapeDtypeStruct((3, bz, bx, n), F32)),
            in_specs=[pl.BlockSpec(memory_space=pltpu.VMEM)],
            out_specs=(pl.BlockSpec(memory_space=pl.ANY), pl.BlockSpec(memory_space=pl.ANY)),
            scratch_shapes=[pltpu.SemaphoreType.DMA((2,))],
        )(pltpu.with_memory_space_constraint(result, pltpu.VMEM))

    in_specs = (
        P(None, "gz", "xy", None), P("gz", "xy", None), P("gz", "xy", None), P("gz", "xy", None),
        P("gz", "xy"), P(), P(), P(), P(),
    )
    out_specs = (P("gz", "xy", None), P(None, "gz", "xy", None))
    return jax.shard_map(body, mesh=mesh, in_specs=in_specs, out_specs=out_specs, check_vma=False)
```

time: 20.9 us -> 18 us (0.86)
  Pallas kernels: 18.9 us -> 17.1 us
  local copies, waits for them, and re-layouts: 1.17 us -> 0 us
    pallas_call x1, Pallas kernels: 18.9 us -> 16.5 us  [body(): pl.pallas_call(functools.partial(kernel, nz, nx, bz, bx, nb, spec, ch, la...]
    pallas_call x0 -> x1, Pallas kernels: none -> 0.62 us  [body(): pl.pallas_call(deliver, out_shape=(jax.ShapeDtypeStruct((bz, bx, n), F32)...]
    slice x1 -> x0, local copies, waits for them, and re-layouts: 0.59 us -> none  [body(): return (result[3], result[:3])]
    squeeze x1 -> x0, local copies, waits for them, and re-layouts: 0.58 us -> none  [body(): return (result[3], result[:3])]
where the time goes in v3:
time: 18 us; the launch traced here: 17.8 us
  Pallas kernels  17.1 us (95%)
  between operations  0.64 us (4%)
    pallas_call x1, Pallas kernels, body(): pl.pallas_call(functools.partial(kernel, nz, nx, bz, bx, nb, spec, ch, la...  16.5 us
    pallas_call x1, Pallas kernels, body(): pl.pallas_call(deliver, out_shape=(jax.ShapeDtypeStruct((bz, bx, n), F32)...  0.62 us

profile of v3, /device:TPU:0, one launch (start us, length us, event | category | flops | bytes accessed | tf_op | source)
XLA Modules:
  0.0 17.8 jit_solution(17397612802700339299)
XLA Ops:
  0.6 16.5 %shard_map.104.result_ref = f32[4,2,2,128]{3,2,1,0:T(2,128)S(1)} custom-call(f32[3,2,2,128]{3,2,1,0:T(2,128)} %coords_hbm.1, s32[2,2,128]{2,1,0:T(2,128)} %species_hbm.1, s32[2,2,128]{2,1,0:T(2,128)} %centers_hbm.1, s32[2,2,128]{2,1,0:T(2,128)} %others_hbm.1, s32[2,2]{1,0:T(2,128)} %live_hbm.1, f32[24,128]{1,0:T(8,128)} %in_hbm.1, f32[32,128]{1,0:T(8,128)} %bitcast.2, ...), custom_call_target="tpu_custom_call" | custom-call | tf_op jit(solution)/shard_map/pallas_call | solution.py:534
  17.2 0.6 %shard_map.105 = (f32[2,2,128]{2,1,0:T(2,128)}, f32[3,2,2,128]{3,2,1,0:T(2,128)}) custom-call(f32[4,2,2,128]{3,2,1,0:T(2,128)S(1)} %shard_map.104.result_ref), custom_call_target="tpu_custom_call" | custom-call | tf_op jit(solution)/shard_map/pallas_call | solution.py:542

commit v4 on v3

--- a/solution.py
+++ b/solution.py
@@ -48,16 +48,20 @@
     nz, nx, bz, bx, nb, spec, ch, lat,
     coords_hbm, species_hbm, centers_hbm, others_hbm, live_hbm, in_hbm, env_hbm, up_hbm, out_hbm,
     result_ref,
-    coords_ref, species_ref, centers_ref, others_ref, live_ref, in_ref, env_ref, up_ref, out_ref,
+    coords_ref, ints_ref, live_ref, weights_ref, out_ref,
     atoms, edges, tab, hot, hot_t, rows_hot, rows_hot_t, codes, rows_c, rows_o, rows_p, rows_live,
     diffs, geo, xs, sins, coss, rad, harm,
     l2, dsilu, wts, feat, dfeat, dlat_own, env_grad, dharm, drad, gr, grad, give_ref, back,
-    send1, recv1, send2, recv2, send3, recv3, load_sem,
+    send_sem, recv_sem, load_sem,
 ):
     n = coords_ref.shape[-1]
     slots = neighbours(nz, nx)
     me_z, me_x = lax.axis_index("gz"), lax.axis_index("xy")
     mine = slots[(1 % nz, 0)]
+    last = len(slots) - 1
+    slots = {key: last if s == mine else mine if s == last else s for key, s in slots.items()}
+    mine = last
+    centre = slots[(0, 0)]
     others_list = [(key, s) for key, s in slots.items() if s != mine]
     index = {s: i for i, (_, s) in enumerate(others_list)}
 
@@ -71,40 +75,41 @@
     for key, _ in others_list:
         pl.semaphore_signal(barrier, inc=1, device_id=owner(key), device_id_type=MESH)
 
-    loads = [
-        pltpu.make_async_copy(source, target, load_sem.at[k])
-        for k, (source, target) in enumerate([
-            (coords_hbm, coords_ref), (species_hbm, species_ref), (centers_hbm, centers_ref),
-            (others_hbm, others_ref), (live_hbm, live_ref), (in_hbm, in_ref), (env_hbm, env_ref),
-            (up_hbm, up_ref), (out_hbm, out_ref)])
-    ]
-    for load in loads:
-        load.start()
-    for load in loads[:5]:
-        load.wait()
+    def whole(ref, sem):
+        pltpu.make_async_copy(ref, ref, sem).wait()
+
+    for k, (source, target) in enumerate([
+            (coords_hbm, coords_ref), (live_hbm, live_ref), (out_hbm, out_ref)]):
+        pltpu.make_async_copy(source, target, load_sem.at[k]).start()
+    for k, source in enumerate((species_hbm, centers_hbm, others_hbm)):
+        pltpu.make_async_copy(source, ints_ref.at[k], load_sem.at[3]).start()
+    rows_in, rows_env, rows_up = in_hbm.shape[0], env_hbm.shape[0], up_hbm.shape[0]
+    row = 0
+    for source in (in_hbm, env_hbm, up_hbm):
+        pltpu.make_async_copy(source, weights_ref.at[pl.ds(row, source.shape[0])], load_sem.at[4]).start()
+        row += source.shape[0]
+    whole(coords_ref, load_sem.at[0])
+    whole(live_ref, load_sem.at[1])
+    whole(ints_ref, load_sem.at[3])
     lane = lax.broadcasted_iota(jnp.int32, (1, n), 1)
     for a in range(bz):
         for b in range(bx):
-            code = centers_ref[a, b : b + 1, :] + 128 * others_ref[a, b : b + 1, :]
+            code = ints_ref[1, a, b : b + 1, :] + 128 * ints_ref[2, a, b : b + 1, :]
             code = jnp.where(lane < live_ref[a : a + 1, b : b + 1], code, -1)
             edges[mine, a, b : b + 1, :] = code.astype(F32)
             atoms[mine, a, b] = jnp.concatenate(
-                [coords_ref[:, a, b, :], species_ref[a, b : b + 1, :].astype(F32)], axis=0)
+                [coords_ref[:, a, b, :], ints_ref[0, a, b : b + 1, :].astype(F32)], axis=0)
     pl.semaphore_wait(barrier, len(others_list))
-    first = {}
     for key, s in others_list:
-        i = index[s]
-        for ref, send, recv in ((atoms, send1, recv1), (edges, send3, recv3)):
-            copy = pltpu.make_async_remote_copy(
-                src_ref=ref.at[mine], dst_ref=ref.at[s], send_sem=send.at[i],
-                recv_sem=recv.at[i], device_id=user(key), device_id_type=MESH,
-            )
-            copy.start()
-            first.setdefault(key, []).append(copy)
-
-    for load in loads[5:]:
-        load.wait()
-    w_in = in_ref[...]
+        for k, ref in enumerate((atoms, edges)):
+            pltpu.make_async_remote_copy(
+                src_ref=ref.at[mine], dst_ref=ref.at[s], send_sem=send_sem.at[k],
+                recv_sem=recv_sem.at[k], device_id=user(key), device_id_type=MESH,
+            ).start()
+
+    whole(out_ref, load_sem.at[2])
+    whole(weights_ref, load_sem.at[4])
+    w_in = weights_ref[:rows_in]
     w_hi = rounded(w_in)
     w_lo = w_in - w_hi
     gap = jnp.zeros((nb, lat), F32)
@@ -116,7 +121,7 @@
     wr2 = jnp.concatenate(
         [jnp.concatenate([w_hi[:nb], w_hi[:nb]], axis=1), jnp.concatenate([w_lo[:nb], gap], axis=1)],
         axis=0).astype(BF16)
-    env_t = env_ref[...]
+    env_t = weights_ref[rows_in : rows_in + rows_env]
     et_hi = rounded(env_t)
     et_lo = env_t - et_hi
     env_t2 = jnp.concatenate(
@@ -126,7 +131,7 @@
     env3 = jnp.concatenate(
         [et_hi, et_hi, et_lo] + ([jnp.zeros((kpad, lat), F32)] if kpad else []), axis=0
     ).T.astype(BF16)
-    up = up_ref[...]
+    up = weights_ref[rows_in + rows_env :]
     up_hi = rounded(up)
     up_lo = up - up_hi
     up3 = jnp.concatenate([up_hi, up_hi, up_lo], axis=1).astype(BF16)
@@ -283,9 +288,10 @@
                     jnp.concatenate([hot_c, hot_c], axis=0)).astype(BF16)
 
     early, late = list(range(2, cz)), [0, 1]
-    for copies in first.values():
-        for copy in copies:
-            copy.wait()
+    for k, ref in enumerate((atoms, edges)):
+        received = ref.at[pl.ds(0, len(others_list))]
+        whole(received, recv_sem.at[k])
+        whole(received, send_sem.at[k])
     every = list(range(cz))
     decode(every)
     tables(range(bz - 2, 2 * bz + 2))
@@ -348,7 +354,7 @@
                     jnp.concatenate([dcl[:, cut], e_lo], axis=0)], axis=1),
                 jnp.concatenate([hot_c, hot_c], axis=0))
             dfeat[:, i * n : (i + 1) * n] += both[: 4 * ch]
-            grad[0, zr - 1, t, 3:4] = -both[4 * ch : 4 * ch + 1]
+            grad[centre, zr - 1, t, 3:4] = -both[4 * ch : 4 * ch + 1]
 
     def backward(rows):
         dms, dls = {}, {}
@@ -438,8 +444,8 @@
                     acc = grad[s, y, x]
                     give_ref[i, y, x] = acc[:4] + acc[4:]
             second[s] = pltpu.make_async_remote_copy(
-                src_ref=give_ref.at[i], dst_ref=back.at[i], send_sem=send2.at[i],
-                recv_sem=recv2.at[i], device_id=owner(key), device_id_type=MESH,
+                src_ref=give_ref.at[i], dst_ref=back.at[i], send_sem=send_sem.at[2],
+                recv_sem=recv_sem.at[2], device_id=owner(key), device_id_type=MESH,
             )
             second[s].start()
 
@@ -460,8 +466,8 @@
         for i in ids_of(zr):
             scatter(i)
     give(set())
-    for copy in second.values():
-        copy.wait()
+    whole(give_ref, send_sem.at[2])
+    whole(back, recv_sem.at[2])
     for a in range(bz):
         for b in range(bx):
             acc = grad[mine, a, b]
@@ -495,7 +501,12 @@
         vmem = lambda shape, dtype=F32: pltpu.VMEM(shape, dtype)
         args = (coords, species, centers, others, live_count, in_weight, env_weight.T, up_weight,
                 out_weight[None])
-        scratch = [vmem(x.shape, x.dtype) for x in args] + [
+        scratch = [
+            vmem(coords.shape),
+            vmem((3, bz, bx, n), jnp.int32),
+            vmem((bz, bx), jnp.int32),
+            vmem((sum(w.shape[0] for w in args[5:8]), lat)),
+            vmem((1, lat)),
             vmem((ns + 1, bz, bx, 4, n)),
             vmem((ns + 1, bz, bx, n)),
             vmem((3 * bz, 3 * bx, 32, n), BF16),
@@ -528,8 +539,10 @@
             vmem((ns + 1, bz, bx, 8, n)),
             vmem((ns, bz, bx, 4, n)),
             vmem((ns, bz, bx, 4, n)),
-        ] + [pltpu.SemaphoreType.DMA((ns,)) for _ in range(6)]
-        scratch.append(pltpu.SemaphoreType.DMA((len(args),)))
+            pltpu.SemaphoreType.DMA((3,)),
+            pltpu.SemaphoreType.DMA((3,)),
+            pltpu.SemaphoreType.DMA((5,)),
+        ]
         specs = [pl.BlockSpec(memory_space=pl.ANY) for _ in args]
         result = pl.pallas_call(
             functools.partial(kernel, nz, nx, bz, bx, nb, spec, ch, lat),

time: 18 us -> 17.7 us (0.983)
  Pallas kernels: 17.1 us -> 16.8 us
    pallas_call x1, Pallas kernels: 16.5 us -> 16.2 us  [body(): pl.pallas_call(functools.partial(kernel, nz, nx, bz, bx, nb, spec, ch, la...]
where the time goes in v4:
time: 17.7 us; the launch traced here: 17.5 us
  Pallas kernels  16.8 us (95%)
  between operations  0.64 us (4%)
    pallas_call x1, Pallas kernels, body(): pl.pallas_call(functools.partial(kernel, nz, nx, bz, bx, nb, spec, ch, la...  16.2 us
    pallas_call x1, Pallas kernels, body(): pl.pallas_call(deliver, out_shape=(jax.ShapeDtypeStruct((bz, bx, n), F32)...  0.62 us

profile of v4, /device:TPU:0, one launch (start us, length us, event | category | flops | bytes accessed | tf_op | source)
XLA Modules:
  0.0 17.5 jit_solution(6868420970453343600)
XLA Ops:
  0.6 16.2 %shard_map.104.result_ref = f32[4,2,2,128]{3,2,1,0:T(2,128)S(1)} custom-call(f32[3,2,2,128]{3,2,1,0:T(2,128)} %coords_hbm.1, s32[2,2,128]{2,1,0:T(2,128)} %species_hbm.1, s32[2,2,128]{2,1,0:T(2,128)} %centers_hbm.1, s32[2,2,128]{2,1,0:T(2,128)} %others_hbm.1, s32[2,2]{1,0:T(2,128)} %live_hbm.1, f32[24,128]{1,0:T(8,128)} %in_hbm.1, f32[32,128]{1,0:T(8,128)} %bitcast.2, ...), custom_call_target="tpu_custom_call" | custom-call | tf_op jit(solution)/shard_map/pallas_call | solution.py:547
  16.9 0.6 %shard_map.105 = (f32[2,2,128]{2,1,0:T(2,128)}, f32[3,2,2,128]{3,2,1,0:T(2,128)}) custom-call(f32[4,2,2,128]{3,2,1,0:T(2,128)S(1)} %shard_map.104.result_ref), custom_call_target="tpu_custom_call" | custom-call | tf_op jit(solution)/shard_map/pallas_call | solution.py:555

commit v5 on v4

--- a/solution.py
+++ b/solution.py
@@ -226,8 +226,13 @@
         rest = 1.0 - q * q
         envelope = rest * rest
         scale = inv * envelope
-        s1 = jnp.sin(math.pi * q)
-        c1 = jnp.cos(math.pi * q)
+        t1 = math.pi * (q - 0.5)
+        t2 = t1 * t1
+        s1, c1 = jnp.ones_like(q), jnp.ones_like(q)
+        for m in range(7, 0, -1):
+            s1 = 1.0 - t2 * s1 * (1.0 / ((2 * m - 1) * (2 * m)))
+            c1 = 1.0 - t2 * c1 * (1.0 / ((2 * m) * (2 * m + 1)))
+        c1 = -t1 * c1
         s0, c0, sk, ck = jnp.zeros_like(s1), jnp.ones_like(c1), s1, c1
         for k in range(nb):
             sins[k, c] = sk
@@ -325,36 +330,45 @@
         d_u = out_rows * (alive * env_row) * (sig + hid * (1.0 - sig))
         dh, dl = split(d_u)
         joins[zr] = dot(up3, jnp.concatenate([dh, dl, dh], axis=0))
+    dcs, dos = {}, {}
     for zr in inner_rows:
         d_join = joins[zr]
         dlat_own[zr - 1] = d_join[:lat]
         d_prod = jnp.concatenate([d_join[lat:]] * 4, axis=0)
-        dch, dcl = split(d_prod * f_os[zr])
-        doh, dol = split(d_prod * f_cs[zr])
-        turned_rows = rows_hot_t[zr - 1]
-        part = dot(jnp.concatenate([doh, dol], axis=1), jnp.concatenate([turned_rows, turned_rows], axis=0))
-        if zr == 1:
-            dfeat[:, : 3 * wide] = part
-            if cz > 3:
-                dfeat[:, 3 * wide :] = jnp.zeros((4 * ch, (cz - 3) * wide), F32)
-        else:
-            dfeat[:, (zr - 1) * wide : (zr + 2) * wide] += part
-        for t, i in enumerate(inner_of(zr)):
-            raw = raws[zr][:, t * n : (t + 1) * n]
-            env_grad[i : i + 1] = raw
-            e_row = raw * geo[3, i : i + 1]
-            e_hi = rounded(e_row)
-            e_lo = jnp.where(row_16 == 0, e_row - e_hi, 0.0).astype(BF16)
-            e_hi = jnp.where(row_16 == 0, e_hi, 0.0).astype(BF16)
-            cut = slice(t * n, (t + 1) * n)
-            hot_c = hot_t[i, :, :n]
-            both = dot(
-                jnp.concatenate([
-                    jnp.concatenate([dch[:, cut], e_hi], axis=0),
-                    jnp.concatenate([dcl[:, cut], e_lo], axis=0)], axis=1),
-                jnp.concatenate([hot_c, hot_c], axis=0))
-            dfeat[:, i * n : (i + 1) * n] += both[: 4 * ch]
-            grad[centre, zr - 1, t, 3:4] = -both[4 * ch : 4 * ch + 1]
+        dcs[zr] = split(d_prod * f_os[zr])
+        dos[zr] = jnp.concatenate(split(d_prod * f_cs[zr]), axis=1)
+
+    def feature_gradient(rows):
+        for r in rows:
+            acc = None
+            for zr in inner_rows:
+                if abs(r - zr) <= 1:
+                    at = r - zr + 1
+                    block = rows_hot_t[zr - 1, :, at * wide : (at + 1) * wide]
+                    term = dot(dos[zr], jnp.concatenate([block, block], axis=0))
+                    acc = term if acc is None else acc + term
+            if r in inner_rows:
+                side = jnp.zeros((4 * ch, n), F32)
+                tops = [side]
+                for t, i in enumerate(inner_of(r)):
+                    cut = slice(t * n, (t + 1) * n)
+                    raw = raws[r][:, cut]
+                    env_grad[i : i + 1] = raw
+                    e_row = raw * geo[3, i : i + 1]
+                    e_hi = rounded(e_row)
+                    e_lo = jnp.where(row_16 == 0, e_row - e_hi, 0.0).astype(BF16)
+                    e_hi = jnp.where(row_16 == 0, e_hi, 0.0).astype(BF16)
+                    hot_c = hot_t[i, :, :n]
+                    dch, dcl = dcs[r]
+                    both = dot(
+                        jnp.concatenate([
+                            jnp.concatenate([dch[:, cut], e_hi], axis=0),
+                            jnp.concatenate([dcl[:, cut], e_lo], axis=0)], axis=1),
+                        jnp.concatenate([hot_c, hot_c], axis=0))
+                    tops.append(both[: 4 * ch])
+                    grad[centre, r - 1, t, 3:4] = -both[4 * ch : 4 * ch + 1]
+                acc = acc + jnp.concatenate(tops + [side], axis=1)
+            dfeat[:, r * wide : (r + 1) * wide] = acc
 
     def backward(rows):
         dms, dls = {}, {}
@@ -454,12 +468,14 @@
             place(cells[i][0] + dz, cells[i][1] + dx)[0]
             for zr in rows for i in ids_of(zr) for dz in (-1, 0, 1) for dx in (-1, 0, 1)}
 
+    feature_gradient(early)
     backward(early[::-1])
     radial_backward(early)
     for zr in reversed(early):
         for i in ids_of(zr):
             scatter(i)
     give(targets(late))
+    feature_gradient(late)
     backward(late[::-1])
     radial_backward(late)
     for zr in reversed(late):

time: 17.7 us -> 17.5 us (0.989)
  no operation moved by 1% of the time
where the time goes in v5:
time: 17.5 us; the launch traced here: 17.4 us
  Pallas kernels  16.7 us (95%)
  between operations  0.64 us (4%)
    pallas_call x1, Pallas kernels, body(): pl.pallas_call(functools.partial(kernel, nz, nx, bz, bx, nb, spec, ch, la...  16.1 us
    pallas_call x1, Pallas kernels, body(): pl.pallas_call(deliver, out_shape=(jax.ShapeDtypeStruct((bz, bx, n), F32)...  0.62 us

profile of v5, /device:TPU:0, one launch (start us, length us, event | category | flops | bytes accessed | tf_op | source)
XLA Modules:
  0.0 17.4 jit_solution(10625752412686317681)
XLA Ops:
  0.6 16.1 %shard_map.104.result_ref = f32[4,2,2,128]{3,2,1,0:T(2,128)S(1)} custom-call(f32[3,2,2,128]{3,2,1,0:T(2,128)} %coords_hbm.1, s32[2,2,128]{2,1,0:T(2,128)} %species_hbm.1, s32[2,2,128]{2,1,0:T(2,128)} %centers_hbm.1, s32[2,2,128]{2,1,0:T(2,128)} %others_hbm.1, s32[2,2]{1,0:T(2,128)} %live_hbm.1, f32[24,128]{1,0:T(8,128)} %in_hbm.1, f32[32,128]{1,0:T(8,128)} %bitcast.2, ...), custom_call_target="tpu_custom_call" | custom-call | tf_op jit(solution)/shard_map/pallas_call | solution.py:563
  16.7 0.6 %shard_map.105 = (f32[2,2,128]{2,1,0:T(2,128)}, f32[3,2,2,128]{3,2,1,0:T(2,128)}) custom-call(f32[4,2,2,128]{3,2,1,0:T(2,128)S(1)} %shard_map.104.result_ref), custom_call_target="tpu_custom_call" | custom-call | tf_op jit(solution)/shard_map/pallas_call | solution.py:571

commit v6 on v5

--- a/solution.py
+++ b/solution.py
@@ -51,7 +51,7 @@
     coords_ref, ints_ref, live_ref, weights_ref, out_ref,
     atoms, edges, tab, hot, hot_t, rows_hot, rows_hot_t, codes, rows_c, rows_o, rows_p, rows_live,
     diffs, geo, xs, sins, coss, rad, harm,
-    l2, dsilu, wts, feat, dfeat, dlat_own, env_grad, dharm, drad, gr, grad, give_ref, back,
+    l2, sigs, lats, wts, feat, dfeat, dlat_own, env_grad, dharm, drad, gr, grad, give_ref, back,
     send_sem, recv_sem, load_sem,
 ):
     n = coords_ref.shape[-1]
@@ -269,7 +269,8 @@
             pre = pres[zr]
             sig = 0.5 + 0.5 * jnp.tanh(0.5 * pre)
             latent = pre * sig
-            dsilu[:, span] = sig + latent * (1.0 - sig)
+            sigs[:, span] = sig
+            lats[:, span] = latent
             lh, ll = split(latent)
             if 1 <= zr <= bz:
                 l2[zr - 1, 0] = lh[:, n : n + inner]
@@ -397,7 +398,8 @@
             if 1 <= zr <= bz:
                 side = jnp.zeros((lat, n), F32)
                 d_lat = d_lat + jnp.concatenate([side, dlat_own[zr - 1], side], axis=1)
-            dh, dl = split(d_lat * dsilu[:, span])
+            sig = sigs[:, span]
+            dh, dl = split(d_lat * (sig + lats[:, span] * (1.0 - sig)))
             d_r = dot(wr2, jnp.concatenate([dh, dl], axis=0))
             d_r = d_r[:nb] + d_r[nb:]
             for t, i in enumerate(ids_of(zr)):
@@ -544,6 +546,7 @@
             vmem((3, cells, n)),
             vmem((bz, 2, lat, bx * n), BF16),
             vmem((lat, cells * n)),
+            vmem((lat, cells * n)),
             vmem((ch, cells * n)),
             vmem((4 * ch, cells * n), BF16),
             vmem((4 * ch, cells * n)),

time: 17.5 us -> 17.5 us (level)
  no operation moved by 1% of the time
where the time goes in v6:
time: 17.5 us; the launch traced here: 17.4 us
  Pallas kernels  16.7 us (95%)
  between operations  0.64 us (4%)
    pallas_call x1, Pallas kernels, body(): pl.pallas_call(functools.partial(kernel, nz, nx, bz, bx, nb, spec, ch, la...  16.1 us
    pallas_call x1, Pallas kernels, body(): pl.pallas_call(deliver, out_shape=(jax.ShapeDtypeStruct((bz, bx, n), F32)...  0.62 us

profile of v6, /device:TPU:0, one launch (start us, length us, event | category | flops | bytes accessed | tf_op | source)
XLA Modules:
  0.0 17.4 jit_solution(13516586777942952319)
XLA Ops:
  0.6 16.1 %shard_map.104.result_ref = f32[4,2,2,128]{3,2,1,0:T(2,128)S(1)} custom-call(f32[3,2,2,128]{3,2,1,0:T(2,128)} %coords_hbm.1, s32[2,2,128]{2,1,0:T(2,128)} %species_hbm.1, s32[2,2,128]{2,1,0:T(2,128)} %centers_hbm.1, s32[2,2,128]{2,1,0:T(2,128)} %others_hbm.1, s32[2,2]{1,0:T(2,128)} %live_hbm.1, f32[24,128]{1,0:T(8,128)} %in_hbm.1, f32[32,128]{1,0:T(8,128)} %bitcast.2, ...), custom_call_target="tpu_custom_call" | custom-call | tf_op jit(solution)/shard_map/pallas_call | solution.py:566
  16.7 0.6 %shard_map.105 = (f32[2,2,128]{2,1,0:T(2,128)}, f32[3,2,2,128]{3,2,1,0:T(2,128)}) custom-call(f32[4,2,2,128]{3,2,1,0:T(2,128)S(1)} %shard_map.104.result_ref), custom_call_target="tpu_custom_call" | custom-call | tf_op jit(solution)/shard_map/pallas_call | solution.py:574
